TPU v7x, 256 devices: a whole 4x4x8 slice. The times are simulated.
256 devices in a mesh: seq: 32 (over x_lo, z, core), head: 8 (over x_hi, y).
Axes of the slice: x: 4 (x_hi: 2, x_lo: 2; x = x_hi * 2 + x_lo), y: 4, z: 8, core: 2. Of those that a mesh axis runs over, the one named last changes fastest.
Arguments:
- hidden: bfloat16 [9216, 8192], P('seq'), may hold values from -6 to 6
- norm_gain: bfloat16 [8192], replicated, may hold values from 0.099609375 to 1.8984375
- w_query: bfloat16 [8192, 4096], P('seq', 'head'), may hold values from -0.125 to 0.125
- w_key: bfloat16 [8192, 1024], P('seq', 'head'), may hold values from -0.125 to 0.125
- w_value: bfloat16 [8192, 1024], P('seq', 'head'), may hold values from -0.0625 to 0.0625
- bias_query: bfloat16 [4096], P('head'), may hold values from -3 to 3
- bias_key: bfloat16 [1024], P('head'), may hold values from -200 to 200
- bias_value: bfloat16 [1024], P('head'), may hold values from -3 to 3
- w_out: bfloat16 [4096, 8192], P('head', 'seq'), may hold values from -0.09375 to 0.09375
Outputs:
- attn_out: bfloat16 [9216, 8192], P(('seq', 'head'))
All inputs are finite; a program needn't handle non-finite values.
Results may differ from a plain program's by a relative error of at most 0.014.
The roundings to bfloat16 on the way count: a program that leaves them out, or rounds other values in their place, can miss the bound.
Values may be sent and summed in bfloat16 or wider, within the bound.
A program may use at most 192 MiB of HBM per device.

v0:
```python
import jax
import jax.numpy as jnp
from jax import lax
from jax.sharding import PartitionSpec as P

HEAD_DIM = 128


ROPE_BASE = 1000000.0
EPSILON = 1e-06


def sent_together(arrays, axis, dim, along):
    widths = [a.shape[along] for a in arrays]
    both = jnp.concatenate(arrays, axis=along)
    result = lax.all_gather(both, axis, axis=dim, tiled=True)
    return tuple(jnp.split(result, [sum(widths[:k]) for k in range(1, len(widths))], axis=along))


def rotary(values, positions):
    half_dim = values.shape[-1] // 2
    freq = ROPE_BASE ** (-2.0 * jnp.arange(half_dim, dtype=jnp.float32) / values.shape[-1])
    angles = positions.astype(jnp.float32)[:, None, None] * freq[None, None, :]
    cosine = jnp.cos(angles)
    sine = jnp.sin(angles)
    first = values[..., :half_dim]
    second = values[..., half_dim:]
    return jnp.concatenate(
        [first * cosine - second * sine, second * cosine + first * sine], axis=-1
    )


def local(hidden, norm_gain, w_query, w_key, w_value, bias_query, bias_key, bias_value, w_out):
    row_count = hidden.shape[0]
    head_count = w_query.shape[1] // HEAD_DIM
    first_row = lax.axis_index("seq") * row_count
    last_row = first_row + row_count - 1
    positions = first_row + jnp.arange(row_count, dtype=jnp.int32)
    widened = hidden.astype(jnp.float32)
    inverse = lax.rsqrt(jnp.mean(widened * widened, axis=-1, keepdims=True) + EPSILON)
    normed = (widened * inverse * norm_gain.astype(jnp.float32)).astype(jnp.bfloat16)
    pieces = sent_together((w_query, w_key, w_value), "seq", 0, 1)
    query = jnp.dot(normed, pieces[0], preferred_element_type=jnp.float32)
    keys = jnp.dot(normed, pieces[1], preferred_element_type=jnp.float32)
    values = jnp.dot(normed, pieces[2], preferred_element_type=jnp.float32)
    query = query + bias_query.astype(jnp.float32)
    keys = keys + bias_key.astype(jnp.float32)
    values = values + bias_value.astype(jnp.float32)
    query = rotary(query.reshape(row_count, head_count, HEAD_DIM), positions).astype(jnp.bfloat16)
    keys = (
        rotary(keys.reshape(row_count, 1, HEAD_DIM), positions)
        .reshape(row_count, HEAD_DIM)
        .astype(jnp.bfloat16)
    )
    values = values.astype(jnp.bfloat16)
    query_heads = query.transpose(1, 0, 2)
    scaling = HEAD_DIM ** (-0.5)
    initial = (
        jnp.full((head_count, row_count), -1e30, jnp.float32),
        jnp.zeros((head_count, row_count), jnp.float32),
        jnp.zeros((head_count, row_count, HEAD_DIM), jnp.float32),
    )
    key_piece, value_piece = sent_together((keys, values), "seq", 0, 1)

    def update(state):
        highest, total, summed = state
        scores = (
            jnp.einsum("hqd,kd->hqk", query_heads, key_piece, preferred_element_type=jnp.float32)
            * scaling
        )
        key_positions = jnp.arange(key_piece.shape[0], dtype=jnp.int32)
        allowed = positions[:, None] >= key_positions[None, :]
        scores = jnp.where(allowed[None], scores, -jnp.inf)
        new_high = jnp.maximum(highest, jnp.max(scores, axis=-1))
        probs = jnp.exp(scores - new_high[..., None])
        total = jnp.sum(probs, axis=-1)
        mixed = jnp.einsum(
            "hqk,kd->hqd",
            probs.astype(jnp.bfloat16),
            value_piece,
            preferred_element_type=jnp.float32,
        )
        return (new_high, total, mixed)

    def unchanged(state):
        return state

    highest, total, summed = lax.cond(jnp.int32(0) <= last_row, update, unchanged, initial)
    attended = (summed / total[..., None]).astype(jnp.bfloat16)
    attended = attended.transpose(1, 0, 2).reshape(row_count, head_count * HEAD_DIM)
    partial_out = jnp.dot(
        attended,
        lax.all_gather(w_out, "seq", axis=1, tiled=True),
        preferred_element_type=jnp.float32,
    )
    result = lax.psum_scatter(
        partial_out.astype(jnp.bfloat16), "head", scatter_dimension=0, tiled=True
    )
    return result


def solution(mesh):
    in_specs = (
        P("seq", None),
        P(),
        P("seq", "head"),
        P("seq", "head"),
        P("seq", "head"),
        P("head"),
        P("head"),
        P("head"),
        P("head", "seq"),
    )
    out_specs = P(("seq", "head"), None)
    return jax.shard_map(local, mesh=mesh, in_specs=in_specs, out_specs=out_specs, check_vma=False)
```

profile of v0, /device:TPU:36, one launch (start us, length us, event | category | flops | bytes accessed | tf_op | source)
XLA Modules:
  0.0 362.3 jit_solution(3323429380837315595)
XLA Ops:
  6.5 1.8 pad_maximum_fusion
  8.4 0.7 convert_element_type.48
  9.1 0.7 convert_element_type.50
  9.8 0.7 convert_element_type.53
  10.5 3.4 fusion.14
  13.8 77.8 %all-gather.4.cloned.1.call-done = bf16[8192,768]{1,0:T(8,128)(2,1)} async-done(((bf16[256,768]{1,0:T(8,128)(2,1)}), bf16[8192,768]{1,0:T(8,128)(2,1)}) %all-gather.4.cloned.1.call-update) | async-done | bytes 12582928 | tf_op jit(solution)/shard_map/all_gather | solution.py:16
  91.6 4.6 %fusion.29 = f32[288,1,128]{2,0,1:T(8,128)S(1)} fusion(bf16[8192,768]{1,0:T(8,128)(2,1)} %all-gather.4.cloned.1.call-done, f32[128]{0:T(128)S(1)} %convert_element_type.50, bf16[288,8192]{1,0:T(8,128)(2,1)} %param.11, f32[8192]{0:T(1024)S(1)} %convert_element_type.48, f32[288]{0:T(512)S(1)} %add_rsqrt_fusion), kind=kOutput, calls=%fused_computation.31 | convolution fusion | flops 613453824 | bytes 6997632 | tf_op jit(solution)/shard_map/dot_general | solution.py:44
  96.2 0.6 fusion.46
  97.0 4.5 %fusion.35 = bf16[288,128]{1,0:T(8,128)(2,1)S(1)} fusion(bf16[8192,768]{1,0:T(8,128)(2,1)} %all-gather.4.cloned.1.call-done, f32[128]{0:T(128)S(1)} %convert_element_type.53, bf16[288,8192]{1,0:T(8,128)(2,1)} %param.11, f32[8192]{0:T(1024)S(1)} %convert_element_type.48, f32[288]{0:T(512)S(1)} %add_rsqrt_fusion), kind=kOutput, calls=%fused_computation.33 | convolution fusion | flops 613490688 | bytes 6923904 | tf_op jit(solution)/shard_map/dot_general | solution.py:45
  101.5 0.7 pad_maximum_fusion.1
  102.3 0.7 all-gather.8.cloned.1.call-update
  103.0 0.6 multiply_cosine_fusion
  103.6 7.5 %fusion.23 = f32[288,512]{1,0:T(8,128)S(1)} fusion(bf16[8192,768]{1,0:T(8,128)(2,1)} %all-gather.4.cloned.1.call-done, f32[512]{0:T(512)S(1)} %convert_element_type.55, bf16[288,8192]{1,0:T(8,128)(2,1)} %param.11, f32[8192]{0:T(1024)S(1)} %convert_element_type.48, f32[288]{0:T(512)S(1)} %add_rsqrt_fusion), kind=kOutput, calls=%fused_computation.29 | convolution fusion | flops 2425503744 | bytes 13732992 | tf_op jit(solution)/shard_map/dot_general | solution.py:43
  111.1 0.2 reshape.160
  111.3 0.4 fusion.52
  111.6 0.2 subtract_convert_fusion
  111.8 0.2 maximum_bitcast_fusion
  112.0 56.9 %all-gather.6.cloned.1.call-done = bf16[9216,256]{1,0:T(8,128)(2,1)} async-done(((bf16[288,256]{1,0:T(8,128)(2,1)}), bf16[9216,256]{1,0:T(8,128)(2,1)}) %all-gather.6.cloned.1.call-update) | async-done | bytes 4718608 | tf_op jit(solution)/shard_map/all_gather | solution.py:16
  168.8 60.1 %conditional.1 = (f32[4,288]{1,0:T(4,128)S(1)}, f32[4,288,128]{2,1,0:T(8,128)S(1)}) conditional(s32[]{:T(128)} %convert_element_type.46, () %tuple.13, (s32[]{:T(128)}, s32[288]{0:T(512)S(1)}, bf16[9216,256]{1,0:T(8,128)(2,1)}, bf16[4,288,128]{2,1,0:T(8,128)(2,1)S(1)}) %tuple.14), branch_computations={%region_1.0_spmd, %region_2.5_spmd} | conditional | flops 5555256832 | bytes 143653264 | solution.py:88
  168.8 1.4 iota_compare_fusion
  170.3 20.0 %fusion.1 = (f32[4,288]{1,0:T(4,128)S(1)}, f32[4,288,9216]{2,1,0:T(8,128)}) fusion(pred[288,9216]{1,0:T(8,128)(4,1)S(1)} %iota_compare_fusion, bf16[4,288,128]{2,1,0:T(8,128)(2,1)S(1)} %get-tuple-element.20, bf16[9216,256]{1,0:T(8,128)(2,1)} %get-tuple-element.21), kind=kOutput, calls=%fused_computation.2 | convolution fusion | flops 2749758464 | bytes 47780352 | tf_op jit(solution)/shard_map/cond/branch_1_fun/hqd,kd->hqk/dot_general | solution.py:68
  190.3 17.9 %fusion.4 = f32[4,288,128]{2,1,0:T(8,128)S(1)} fusion(f32[4,288,9216]{2,1,0:T(8,128)} %get-tuple-element.27, f32[4,288]{1,0:T(4,128)S(1)} %broadcast_maximum_fusion, pred[288,9216]{1,0:T(8,128)(4,1)S(1)} %iota_compare_fusion, bf16[9216,256]{1,0:T(8,128)(2,1)} %get-tuple-element.21), kind=kOutput, calls=%fused_computation.5 | convolution fusion | flops 2760376320 | bytes 48075264 | tf_op jit(solution)/shard_map/cond/branch_1_fun/hqk,kd->hqd/dot_general | solution.py:77
  208.3 20.7 %fusion.3 = f32[4,288]{1,0:T(4,128)S(1)} fusion(f32[4,288,9216]{2,1,0:T(8,128)} %get-tuple-element.27, f32[4,288]{1,0:T(4,128)S(1)} %broadcast_maximum_fusion, pred[288,9216]{1,0:T(8,128)(4,1)S(1)} %iota_compare_fusion), kind=kLoop, calls=%fused_computation.4 | loop fusion | flops 42466176 | bytes 45130752 | tf_op jit(solution)/shard_map/cond/branch_1_fun/reduce_sum | solution.py:76
  229.0 31.2 %all-gather.8.cloned.1.call-done = bf16[512,8192]{1,0:T(8,128)(2,1)} async-done(((bf16[512,256]{1,0:T(8,128)(2,1)}), bf16[512,8192]{1,0:T(8,128)(2,1)}) %all-gather.8.cloned.1.call-update) | async-done | bytes 8388624 | tf_op jit(solution)/shard_map/all_gather | solution.py:93
  260.1 7.7 %convolution_convert_fusion = bf16[288,8192]{1,0:T(8,128)(2,1)} fusion(bf16[512,8192]{1,0:T(8,128)(2,1)} %all-gather.8.cloned.1.call-done, f32[4,288,128]{2,1,0:T(8,128)S(1)} %get-tuple-element.24, f32[4,288]{1,0:T(4,128)S(1)} %get-tuple-element.25), kind=kOutput, calls=%fused_computation.19 | convolution fusion | flops 2418573312 | bytes 13701632 | tf_op jit(solution)/shard_map/dot_general | solution.py:91
  267.9 67.7 %fusion = bf16[40,8192]{1,0:T(8,128)(2,1)S(1)} fusion(bf16[288,8192]{1,0:T(8,128)(2,1)} %convolution_convert_fusion), kind=kCustom, calls=%all-reduce-scatter | all-reduce-scatter fusion | flops 2621441 | bytes 5374976
  335.6 0.1 slice.20
  335.7 1.9 collective-permute-start
  337.6 0.6 dynamic-slice.4
  338.9 15.0 %collective-permute-done = bf16[28,8192]{1,0:T(8,128)(2,1)S(1)} collective-permute-done((bf16[28,8192]{1,0:T(8,128)(2,1)S(1)}, bf16[28,8192]{1,0:T(8,128)(2,1)S(1)}, u32[]{:S(2)}, u32[]{:S(2)}) %collective-permute-start) | collective-permute-done | bytes 458784
  353.8 0.9 concatenate.18
  354.8 1.0 constant_dynamic-slice_fusion
  (17 shorter events, 0.3 us)
Async XLA Ops:
  6.5 85.1 %all-gather.4.cloned.1.call-start = ((), (), s32[]{:S(2)}) async-start(), calls=%async_computation | async-start | bytes 12976128 | tf_op jit(solution)/shard_map/all_gather | solution.py:16
  8.4 160.5 %all-gather.6.cloned.1.call-start = ((), (), s32[]{:S(2)}) async-start(), calls=%async_computation.1 | async-start | bytes 4866048 | tf_op jit(solution)/shard_map/all_gather | solution.py:16
  96.2 6.7 %copy-start = (bf16[512]{0:T(512)(128)(2,1)S(1)}, bf16[512]{0:T(512)(128)(2,1)}, u32[]{:S(2)}) copy-start(bf16[512]{0:T(512)(128)(2,1)} %param.16) | copy-start | bytes 3076
  102.2 157.9 %all-gather.8.cloned.1.call-start = ((), (), s32[]{:S(2)}) async-start(), calls=%async_computation.2 | async-start | bytes 8650752 | tf_op jit(solution)/shard_map/all_gather | solution.py:93
  260.1 77.5 %copy-start.1 = (u32[256]{0:T(256)S(1)}, u32[256]{0:T(256)}, u32[]{:S(2)}) copy-start(u32[256]{0:T(256)} %constant.41) | copy-start | bytes 3076
  335.7 18.2 %collective-permute-start = (bf16[28,8192]{1,0:T(8,128)(2,1)S(1)}, bf16[28,8192]{1,0:T(8,128)(2,1)S(1)}, u32[]{:S(2)}, u32[]{:S(2)}) collective-permute-start(bf16[28,8192]{1,0:T(8,128)(2,1)S(1)} %slice.20), channel_id=1, source_target_pairs={{0,1},{1,2},{2,3},{3,4},{4,5},{5,6},{6,7},{8,9},{9,10},{10,11},{11... | collective-permute-start | bytes 1376264
Sparse Core Ops, SparseCore 0:
  9.2 82.4 all-gather.3
  102.3 66.4 all-gather.5
  170.6 89.4 all-gather.7
where the time goes:
time: 363 us; the launch traced here: 362 us
  waiting for transfers between devices  182 us (50%)
  blocking collectives  67.7 us (19%)
  matrix products  62.2 us (17%)
  other arithmetic  31.7 us (9%)
  between operations  13.9 us (4%)
    all_gather x2, waiting for transfers between devices, sent_together(): result = lax.all_gather(both, axis, axis=dim, tiled=True)  135 us
    unnamed x1, blocking collectives  67.7 us
    all_gather x1, waiting for transfers between devices, local(): lax.all_gather(w_out, 'seq', axis=1, tiled=True)  31.2 us
    reduce_sum x1, other arithmetic, update(): total = jnp.sum(probs, axis=-1)  20.7 us
    dot_general x1, matrix products, update(): jnp.einsum('hqd,kd->hqk', query_heads, key_piece, preferred_element_type=...  20 us
    dot_general x1, matrix products, update(): jnp.einsum('hqk,kd->hqd', probs.astype(jnp.bfloat16), value_piece, prefer...  17.9 us
    unnamed x4, waiting for transfers between devices  15.7 us
    dot_general x1, matrix products, local(): jnp.dot(attended, lax.all_gather(w_out, 'seq', axis=1, tiled=True), prefe...  7.73 us
  transfers between devices with their start and end apart: 4, of which 4 were waited for; matrix products, arithmetic and copies ran while one was open for 21% of the time, Pallas kernels for 0%

commit v1 on v0

v1 whole, which is shorter than its diff:
```python
import functools

import jax
import jax.numpy as jnp
from jax import lax
from jax.experimental import pallas as pl
from jax.experimental.pallas import tpu as pltpu
from jax.sharding import PartitionSpec as P

HEAD_DIM = 128
ROPE_BASE = 1000000.0
EPSILON = 1e-06
BF16 = jnp.bfloat16
F32 = jnp.float32
MESH = pl.DeviceIdType.MESH
ZS = 8
YS = 4
SEQ = 32
ROWS = 288
D = 8192
OWN = 36
GROUPS = 4
GCOLS = D // GROUPS
KBLOCK = 1152
PADROWS = 80
SCALE2 = HEAD_DIM**-0.5 * 1.4426950408889634


def wrap(value, size):
    return lax.rem(value + size, size)


class Gather:
    def __init__(self, kind, buf, rows, place, recv, sib_sem, send_sem):
        self.kind, self.buf, self.rows, self.half = kind, buf, rows, rows // 2
        self.x, self.z, self.c, self.head = place
        self.recv, self.sib_sem, self.send_sem = recv, sib_sem, send_sem
        self.zp = self.at(self.x, 1)
        self.zm = self.at(self.x, -1)
        self.xp = self.at(1 - self.x, 0)
        self.sib = (self.x * ZS + self.z) * 2 + 1 - self.c

    def at(self, x, dz):
        return (x * ZS + wrap(self.z + dz, ZS)) * 2 + self.c

    def copy(self, s, part, dev, sem):
        ref = self.buf.at[pl.ds(pl.multiple_of(s * self.rows + part * self.half, 16), self.half)]
        return pltpu.make_async_remote_copy(
            src_ref=ref,
            dst_ref=ref,
            send_sem=self.send_sem.at[self.kind],
            recv_sem=sem,
            device_id=(dev, self.head),
            device_id_type=MESH,
        )

    def sem(self, s, part):
        return self.recv.at[self.kind, lax.div(s, 2), part]

    def send(self, s, part, *devs):
        for dev in devs:
            self.copy(s, part, dev, self.sem(s, part)).start()
        self.copy(s, part, self.sib, self.sib_sem.at[self.kind]).start()

    def wait(self, s, part):
        self.copy(s, part, self.sib, self.sem(s, part)).wait_recv()

    def relay(self, s, part, *devs):
        self.wait(s, part)
        self.send(s, part, *devs)

    def own(self):
        s = self.at(self.x, 0)
        for part in (0, 1):
            self.send(s, part, self.zp, self.zm, self.xp)

    def cross(self):
        s = self.at(1 - self.x, 0)
        self.relay(s, 0, self.zp, self.zm)
        self.relay(s, 1)

    def step(self, k):
        lo, hi = self.at(self.x, -k), self.at(self.x, k)
        self.relay(lo, 0, self.zp)
        self.relay(hi, 0, self.zm)
        self.relay(lo, 1, self.zp, self.xp)
        self.relay(hi, 1, self.zm, self.xp)
        self.relay(self.at(1 - self.x, -k), 0, self.zp)
        self.relay(self.at(1 - self.x, k), 0, self.zm)

    def crossed(self, k):
        self.relay(self.at(1 - self.x, -k), 1)
        self.relay(self.at(1 - self.x, k), 1)

    def step3(self):
        lo, hi = self.at(self.x, -3), self.at(self.x, 3)
        self.relay(lo, 0, self.zp)
        self.relay(hi, 1, self.zm, self.xp)
        self.relay(lo, 1, self.xp)
        self.relay(hi, 0)
        self.relay(self.at(1 - self.x, -3), 0)
        self.relay(self.at(1 - self.x, 3), 0)

    def step4(self):
        far = self.at(self.x, 4)
        self.relay(far, 0, self.xp)
        self.relay(far, 1, self.xp)

    def last(self):
        far = self.at(1 - self.x, 4)
        self.relay(far, 0)
        self.relay(far, 1)

    def finish(self):
        part = self.buf.at[pl.ds(0, 16 * self.rows)]
        pltpu.make_async_copy(part, part, self.sib_sem.at[self.kind]).wait()

    def drain(self):
        part = self.buf.at[pl.ds(0, 31 * self.rows)]
        pltpu.make_async_copy(part, part, self.send_sem.at[self.kind]).wait()


def rotated(values, cs, sn):
    return values * cs + pltpu.roll(values, HEAD_DIM // 2, 1) * sn


def kernel(
    hidden, gain, wq_in, wk_in, wv_in, bq, bk, bv, wo_in, cs, sn, out,
    hid, wkv, wq, kv, wo, qacc, qs, tmp, att32, att, terms, r1, r2, xs, xr, tot, keep,
    local, recv, sib_sem, send_sem, rsem, r_send,
):
    s = lax.axis_index("seq")
    head = lax.axis_index("head")
    c = lax.rem(s, 2)
    chip = lax.div(s, 2)
    z = lax.rem(chip, ZS)
    x = lax.div(chip, ZS)
    y = lax.rem(head, YS)
    xh = lax.div(head, YS)
    place = (x, z, c, head)
    gather = functools.partial(Gather, place=place, recv=recv, sib_sem=sib_sem, send_sem=send_sem)
    g_kv_w = gather(0, wkv, 256)
    g_q_w = gather(1, wq, 256)
    g_kv = gather(2, kv, ROWS)
    g_o_w = gather(3, wo, 512)
    yp = xh * YS + wrap(y + 1, YS)
    ym = xh * YS + wrap(y - 1, YS)
    xhp = (1 - xh) * YS + y

    mine = pl.ds(pl.multiple_of(s * 256, 256), 256)
    mine_o = pl.ds(pl.multiple_of(s * 512, 512), 512)
    copies = [
        pltpu.make_async_copy(wk_in, wkv.at[mine, pl.ds(0, 128)], local.at[0]),
        pltpu.make_async_copy(wv_in, wkv.at[mine, pl.ds(128, 128)], local.at[1]),
        pltpu.make_async_copy(wq_in, wq.at[mine], local.at[2]),
        pltpu.make_async_copy(hidden, hid, local.at[3]),
        pltpu.make_async_copy(wo_in, wo.at[mine_o], local.at[4]),
    ]
    for copy in copies:
        copy.start()
    barrier = pltpu.get_barrier_semaphore()
    for dev in (g_q_w.zp, g_q_w.zm, g_q_w.xp, g_q_w.sib):
        pl.semaphore_signal(barrier, inc=1, device_id=(dev, head), device_id_type=MESH)
    for dev in (yp, ym, xhp):
        pl.semaphore_signal(barrier, inc=1, device_id=(s, dev), device_id_type=MESH)
    copies[0].wait()
    copies[1].wait()
    copies[2].wait()
    pl.semaphore_wait(barrier, 7)
    g_kv_w.own()
    g_q_w.own()

    copies[3].wait()

    @pl.loop(0, ROWS // 16)
    def _(i):
        rows = pl.ds(pl.multiple_of(i * 16, 16), 16)
        squares = jnp.zeros((16, 1024), F32)
        for j in range(8):
            part = hid[rows, pl.ds(j * 1024, 1024)].astype(F32)
            squares = squares + part * part
        inverse = lax.rsqrt(jnp.sum(squares, axis=-1, keepdims=True) * (1.0 / D) + EPSILON)
        for j in range(8):
            cols = pl.ds(j * 1024, 1024)
            part = hid[rows, cols].astype(F32)
            hid[rows, cols] = (part * inverse * gain[:, cols].astype(F32)).astype(BF16)

    def steps12(g):
        @pl.loop(1, 3)
        def _(k):
            g.step(k)

            @pl.when(k == 2)
            def _():
                g.crossed(1)

    def tail(g):
        g.step3()
        g.crossed(2)
        g.step4()
        g.crossed(3)
        g.last()

    g_kv_w.cross()
    steps12(g_kv_w)
    tail(g_kv_w)
    g_q_w.cross()
    g_kv_w.finish()

    def project(weights, cols):
        acc = qacc.at[:, pl.ds(0, cols)]
        acc[...] = jnp.zeros((ROWS, cols), F32)

        @pl.loop(0, 4)
        def _(i):
            depth = pl.ds(pl.multiple_of(i * 2048, 2048), 2048)
            acc[...] += jnp.dot(hid[:, depth], weights[depth, :], preferred_element_type=F32)

    project(wkv, 256)
    own_kv = pl.ds(pl.multiple_of(s * ROWS, 16), ROWS)
    kv[own_kv, 0:128] = rotated(qacc[:, 0:128] + bk[...].astype(F32), cs[...], sn[...]).astype(BF16)
    kv[own_kv, 128:256] = (qacc[:, 128:256] + bv[...].astype(F32)).astype(BF16)
    g_q_w.step(1)
    g_kv.own()
    g_q_w.step(2)
    g_q_w.crossed(1)
    g_kv.cross()
    g_q_w.step3()
    g_q_w.crossed(2)
    g_kv.step(1)
    g_q_w.step4()
    g_q_w.crossed(3)
    g_kv.step(2)
    g_kv.crossed(1)
    g_q_w.last()
    tail(g_kv)
    copies[4].wait()
    g_o_w.own()
    g_q_w.finish()
    project(wq, 512)
    for j in range(4):
        cols = pl.ds(j * HEAD_DIM, HEAD_DIM)
        value = qacc[:, cols] + bq[:, cols].astype(F32)
        qs[pl.ds(j * ROWS, ROWS), :] = rotated(value, cs[...], sn[...]).astype(BF16)
    g_kv.finish()
    g_o_w.cross()

    last_block = lax.div(s, 4)
    att32[...] = jnp.zeros(att32.shape, F32)

    @pl.loop(0, 4)
    def _(j):
        query = qs[pl.ds(pl.multiple_of(j * ROWS, 16), ROWS), :]

        def scores_of(block):
            keys = kv[pl.ds(pl.multiple_of(block * KBLOCK, KBLOCK), KBLOCK), 0:128]
            return lax.dot_general(query, keys, (((1,), (1,)), ((), ())), preferred_element_type=F32)

        def mixed(probs, block):
            values = kv[pl.ds(pl.multiple_of(block * KBLOCK, KBLOCK), KBLOCK), 128:256]
            return jnp.dot(probs.astype(BF16), values, preferred_element_type=F32)

        scores = scores_of(last_block)
        query_pos = s * ROWS + lax.broadcasted_iota(jnp.int32, (ROWS, KBLOCK), 0)
        key_pos = last_block * KBLOCK + lax.broadcasted_iota(jnp.int32, (ROWS, KBLOCK), 1)
        scores = jnp.where(query_pos >= key_pos, scores, -jnp.inf)
        highest = jnp.max(scores, axis=-1, keepdims=True)
        probs = jnp.exp2((scores - highest) * SCALE2)
        total = jnp.sum(probs, axis=-1, keepdims=True)
        summed = mixed(probs, last_block)

        def update(block, state):
            highest, total, summed = state
            scores = scores_of(block)
            new_high = jnp.maximum(highest, jnp.max(scores, axis=-1, keepdims=True))
            probs = jnp.exp2((scores - new_high) * SCALE2)
            fade = jnp.exp2((highest - new_high) * SCALE2)
            total = total * fade + jnp.sum(probs, axis=-1, keepdims=True)
            return new_high, total, summed * fade + mixed(probs, block)

        highest, total, summed = lax.fori_loop(0, last_block, update, (highest, total, summed))
        tmp[...] = summed / total
        cols = pl.ds(pl.multiple_of(j * HEAD_DIM, HEAD_DIM), HEAD_DIM)
        for h in range(8):
            spot = PADROWS * (h % YS) + OWN * (h // YS)
            att32[pl.ds(spot, OWN), cols] = tmp[pl.ds(h * OWN, OWN), :]

        @pl.when(j < 2)
        def _():
            g_o_w.step(j + 1)

        @pl.when(j == 2)
        def _():
            g_o_w.crossed(1)
            g_o_w.step3()

        @pl.when(j == 3)
        def _():
            g_o_w.crossed(2)
            g_o_w.step4()

    att[...] = att32[...].astype(BF16)
    g_o_w.crossed(3)
    g_o_w.last()
    g_o_w.finish()

    y2 = wrap(y + 2, YS)
    y_next = wrap(y + 1, YS)
    y_prev = wrap(y - 1, YS)
    half_cols = GCOLS // 2

    def move(src, dst, kind, g, dev):
        return pltpu.make_async_remote_copy(
            src_ref=src,
            dst_ref=dst,
            send_sem=r_send.at[kind, g],
            recv_sem=rsem.at[kind, g],
            device_id=(s, dev),
            device_id_type=MESH,
        )

    def first(g, kind):
        cols = pl.ds(g * GCOLS + kind * half_cols, half_cols)
        return move(terms.at[y2, :, cols], r1.at[kind, g], kind, g, ym if kind else yp)

    def second(g, kind):
        cols = pl.ds(g * GCOLS, GCOLS)
        row = y_prev if kind else y_next
        return move(terms.at[row, :, cols], r2.at[kind, g], 2 + kind, g, ym if kind else yp)

    def third(g):
        return move(xs.at[g], xr.at[g], 4, g, xhp)

    def compute(g):
        @pl.loop(0, GCOLS // 256)
        def _(i):
            slot = g * (GCOLS // 256) + i
            depth = pl.ds(pl.multiple_of(slot * 512, 512), 512)
            cols = pl.ds(pl.multiple_of(slot * 256, 256), 256)
            term = jnp.dot(att[...], wo[depth, :], preferred_element_type=F32).astype(BF16)
            for k in range(YS):
                terms[k, :, cols] = term[PADROWS * k : PADROWS * k + 2 * OWN]

        first(g, 0).start()
        first(g, 1).start()

    def pair(g):
        for kind in (0, 1):
            first(g, kind).wait_recv()
            row = y_prev if kind else y_next
            cols = pl.ds(g * GCOLS + kind * half_cols, half_cols)
            terms[row, :, cols] = (terms[row, :, cols].astype(F32) + r1[kind, g].astype(F32)).astype(BF16)
            second(g, kind).start()

    def across(g):
        second(g, 0).wait_recv()
        second(g, 1).wait_recv()
        cols = pl.ds(g * GCOLS, GCOLS)
        tot[...] = terms[y, :, cols].astype(F32) + r2[0, g].astype(F32) + r2[1, g].astype(F32)
        low, high = tot[0:OWN, :], tot[OWN : 2 * OWN, :]
        lower = xh == 0
        xs[g] = jnp.where(lower, high, low).astype(BF16)
        keep[g] = jnp.where(lower, low, high)
        third(g).start()

    def done(g):
        third(g).wait_recv()
        out[:, pl.ds(g * GCOLS, GCOLS)] = (keep[g] + xr[g].astype(F32)).astype(BF16)

    for t in range(GROUPS + 3):
        for lag, stage in enumerate((compute, pair, across, done)):
            if 0 <= t - lag < GROUPS:
                stage(t - lag)

    for g in range(GROUPS):
        for kind in (0, 1):
            first(g, kind).wait_send()
            second(g, kind).wait_send()
        third(g).wait_send()
    for g in (g_kv_w, g_q_w, g_kv, g_o_w):
        g.drain()


def local(hidden, norm_gain, w_query, w_key, w_value, bias_query, bias_key, bias_value, w_out):
    first_row = lax.axis_index("seq") * ROWS
    positions = first_row + jnp.arange(ROWS, dtype=jnp.int32)
    half_dim = HEAD_DIM // 2
    freq = ROPE_BASE ** (-2.0 * jnp.arange(half_dim, dtype=F32) / HEAD_DIM)
    angles = positions.astype(F32)[:, None] * freq[None, :]
    cosine, sine = jnp.cos(angles), jnp.sin(angles)
    cs = jnp.concatenate([cosine, cosine], axis=-1)
    sn = jnp.concatenate([-sine, sine], axis=-1)
    vmem = pl.BlockSpec(memory_space=pltpu.VMEM)
    hbm = pl.BlockSpec(memory_space=pl.ANY)
    dma = pltpu.SemaphoreType.DMA
    return pl.pallas_call(
        kernel,
        name="layer",
        out_shape=jax.ShapeDtypeStruct((OWN, D), BF16),
        in_specs=[hbm, vmem, hbm, hbm, hbm, vmem, vmem, vmem, hbm, vmem, vmem],
        out_specs=vmem,
        scratch_shapes=[
            pltpu.VMEM((ROWS, D), BF16),
            pltpu.VMEM((D, 256), BF16),
            pltpu.VMEM((D, 512), BF16),
            pltpu.VMEM((SEQ * ROWS, 256), BF16),
            pltpu.VMEM((SEQ * 512, 256), BF16),
            pltpu.VMEM((ROWS, 512), F32),
            pltpu.VMEM((4 * ROWS, HEAD_DIM), BF16),
            pltpu.VMEM((ROWS, HEAD_DIM), F32),
            pltpu.VMEM((YS * PADROWS, 512), F32),
            pltpu.VMEM((YS * PADROWS, 512), BF16),
            pltpu.VMEM((YS, 2 * OWN, D), BF16),
            pltpu.VMEM((2, GROUPS, 2 * OWN, GCOLS // 2), BF16),
            pltpu.VMEM((2, GROUPS, 2 * OWN, GCOLS), BF16),
            pltpu.VMEM((GROUPS, OWN, GCOLS), BF16),
            pltpu.VMEM((GROUPS, OWN, GCOLS), BF16),
            pltpu.VMEM((2 * OWN, GCOLS), F32),
            pltpu.VMEM((GROUPS, OWN, GCOLS), F32),
            dma((5,)),
            dma((4, 16, 2)),
            dma((4,)),
            dma((4,)),
            dma((5, GROUPS)),
            dma((5, GROUPS)),
        ],
        compiler_params=pltpu.CompilerParams(
            collective_id=0, has_side_effects=True, vmem_limit_bytes=66 * 1000 * 1000
        ),
    )(
        hidden, norm_gain.reshape(1, D), w_query, w_key, w_value, bias_query.reshape(1, 512),
        bias_key.reshape(1, 128), bias_value.reshape(1, 128), w_out, cs, sn,
    )


def solution(mesh):
    in_specs = (
        P("seq", None),
        P(),
        P("seq", "head"),
        P("seq", "head"),
        P("seq", "head"),
        P("head"),
        P("head"),
        P("head"),
        P("head", "seq"),
    )
    out_specs = P(("seq", "head"), None)
    return jax.shard_map(local, mesh=mesh, in_specs=in_specs, out_specs=out_specs, check_vma=False)
```

time: 363 us -> 191 us (0.53)
  the two profiles are of different devices: /device:TPU:36 before, /device:TPU:1 now
where the time goes in v1:
time: 191 us
  Pallas kernels  185 us (97%)
  local copies, waits for them, and re-layouts  4.57 us (2%)
    pallas_call x1, Pallas kernels, local(): pl.pallas_call(kernel, name='layer', out_shape=jax.ShapeDtypeStruct((OWN,...  185 us

profile of v1, /device:TPU:1, one launch (start us, length us, event | category | flops | bytes accessed | tf_op | source)
XLA Modules:
  0.0 190.6 jit_solution(11519647473143952445)
XLA Ops:
  0.0 1.3 reshape.23.bq
  1.3 1.3 reshape.22.gain
  2.6 0.6 fusion
  3.2 0.8 pad_maximum_fusion
  4.1 184.6 %layer.1 = bf16[36,8192]{1,0:T(8,128)(2,1)} custom-call(bf16[288,8192]{1,0:T(8,128)(2,1)} %hidden.1, bf16[1,8192]{1,0:T(2,128)(2,1)} %reshape.22.gain, bf16[256,512]{1,0:T(8,128)(2,1)} %wq_in.1, bf16[256,128]{1,0:T(8,128)(2,1)} %wk_in.1, bf16[256,128]{1,0:T(8,128)(2,1)} %wv_in.1, bf16[1,512]{1,0:T(2,128)(2,1)} %reshape.23.bq, bf16[1,128]{1,0:T(2,128)(2,1)} %bitcast.2, ...), custom_call_target="tpu_custom_call" | custom-call | tf_op jit(solution)/shard_map/layer/pallas_call | solution.py:396
  188.7 2.0 %copy.11 = bf16[36,8192]{1,0:T(8,128)(2,1)} copy(bf16[36,8192]{1,0:T(8,128)(2,1)} %layer.1) | data formatting | bytes 1179648
  (2 shorter events, 0.0 us)

commit v2 on v1

--- a/solution.py
+++ b/solution.py
@@ -19,8 +19,9 @@
 ROWS = 288
 D = 8192
 OWN = 36
-GROUPS = 4
-GCOLS = D // GROUPS
+GROUPS = 5
+COLS = (1024, 2048, 2048, 2048, 1024)
+BASE = (0, 1024, 3072, 5120, 7168)
 KBLOCK = 1152
 PADROWS = 80
 SCALE2 = HEAD_DIM**-0.5 * 1.4426950408889634
@@ -57,63 +58,72 @@
     def sem(self, s, part):
         return self.recv.at[self.kind, lax.div(s, 2), part]
 
-    def send(self, s, part, *devs):
+    def send(self, k, s, part, *devs):
         for dev in devs:
             self.copy(s, part, dev, self.sem(s, part)).start()
-        self.copy(s, part, self.sib, self.sib_sem.at[self.kind]).start()
-
-    def wait(self, s, part):
+        self.copy(s, part, self.sib, self.sib_sem.at[self.kind, k]).start()
+
+    def relay(self, k, s, part, *devs):
         self.copy(s, part, self.sib, self.sem(s, part)).wait_recv()
-
-    def relay(self, s, part, *devs):
-        self.wait(s, part)
-        self.send(s, part, *devs)
+        self.send(k, s, part, *devs)
 
     def own(self):
         s = self.at(self.x, 0)
         for part in (0, 1):
-            self.send(s, part, self.zp, self.zm, self.xp)
+            self.send(0, s, part, self.zp, self.zm, self.xp)
 
     def cross(self):
         s = self.at(1 - self.x, 0)
-        self.relay(s, 0, self.zp, self.zm)
-        self.relay(s, 1)
+        self.relay(0, s, 0, self.zp, self.zm)
+        self.relay(0, s, 1)
+
+    def step_a(self, k):
+        self.relay(k, self.at(self.x, -k), 0, self.zp)
+        self.relay(k, self.at(self.x, k), 0, self.zm)
+
+    def step_b(self, k):
+        self.relay(k, self.at(self.x, -k), 1, self.zp, self.xp)
+        self.relay(k, self.at(self.x, k), 1, self.zm, self.xp)
+
+    def step_c(self, k):
+        self.relay(k, self.at(1 - self.x, -k), 0, self.zp)
+        self.relay(k, self.at(1 - self.x, k), 0, self.zm)
 
     def step(self, k):
-        lo, hi = self.at(self.x, -k), self.at(self.x, k)
-        self.relay(lo, 0, self.zp)
-        self.relay(hi, 0, self.zm)
-        self.relay(lo, 1, self.zp, self.xp)
-        self.relay(hi, 1, self.zm, self.xp)
-        self.relay(self.at(1 - self.x, -k), 0, self.zp)
-        self.relay(self.at(1 - self.x, k), 0, self.zm)
+        self.step_a(k)
+        self.step_b(k)
+        self.step_c(k)
 
     def crossed(self, k):
-        self.relay(self.at(1 - self.x, -k), 1)
-        self.relay(self.at(1 - self.x, k), 1)
+        self.relay(k, self.at(1 - self.x, -k), 1)
+        self.relay(k, self.at(1 - self.x, k), 1)
 
     def step3(self):
         lo, hi = self.at(self.x, -3), self.at(self.x, 3)
-        self.relay(lo, 0, self.zp)
-        self.relay(hi, 1, self.zm, self.xp)
-        self.relay(lo, 1, self.xp)
-        self.relay(hi, 0)
-        self.relay(self.at(1 - self.x, -3), 0)
-        self.relay(self.at(1 - self.x, 3), 0)
+        self.relay(3, lo, 0, self.zp)
+        self.relay(3, hi, 1, self.zm, self.xp)
+        self.relay(3, lo, 1, self.xp)
+        self.relay(3, hi, 0)
+        self.relay(3, self.at(1 - self.x, -3), 0)
+        self.relay(3, self.at(1 - self.x, 3), 0)
 
     def step4(self):
         far = self.at(self.x, 4)
-        self.relay(far, 0, self.xp)
-        self.relay(far, 1, self.xp)
+        self.relay(4, far, 0, self.xp)
+        self.relay(4, far, 1, self.xp)
 
     def last(self):
         far = self.at(1 - self.x, 4)
-        self.relay(far, 0)
-        self.relay(far, 1)
+        self.relay(4, far, 0)
+        self.relay(4, far, 1)
+
+    def sibling(self, k):
+        part = self.buf.at[pl.ds(0, (2 if k in (0, 4) else 4) * self.rows)]
+        pltpu.make_async_copy(part, part, self.sib_sem.at[self.kind, k]).wait()
 
     def finish(self):
-        part = self.buf.at[pl.ds(0, 16 * self.rows)]
-        pltpu.make_async_copy(part, part, self.sib_sem.at[self.kind]).wait()
+        for k in range(5):
+            self.sibling(k)
 
     def drain(self):
         part = self.buf.at[pl.ds(0, 31 * self.rows)]
@@ -127,6 +137,7 @@
 def kernel(
     hidden, gain, wq_in, wk_in, wv_in, bq, bk, bv, wo_in, cs, sn, out,
     hid, wkv, wq, kv, wo, qacc, qs, tmp, att32, att, terms, r1, r2, xs, xr, tot, keep,
+    scores0, scores1, high, acc,
     local, recv, sib_sem, send_sem, rsem, r_send,
 ):
     s = lax.axis_index("seq")
@@ -185,16 +196,7 @@
             part = hid[rows, cols].astype(F32)
             hid[rows, cols] = (part * inverse * gain[:, cols].astype(F32)).astype(BF16)
 
-    def steps12(g):
-        @pl.loop(1, 3)
-        def _(k):
-            g.step(k)
-
-            @pl.when(k == 2)
-            def _():
-                g.crossed(1)
-
-    def tail(g):
+    def stages(g):
         g.step3()
         g.crossed(2)
         g.step4()
@@ -202,9 +204,12 @@
         g.last()
 
     g_kv_w.cross()
-    steps12(g_kv_w)
-    tail(g_kv_w)
+    g_kv_w.step(1)
     g_q_w.cross()
+    g_kv_w.step(2)
+    g_kv_w.crossed(1)
+    g_q_w.step(1)
+    stages(g_kv_w)
     g_kv_w.finish()
 
     def project(weights, cols):
@@ -220,94 +225,99 @@
     own_kv = pl.ds(pl.multiple_of(s * ROWS, 16), ROWS)
     kv[own_kv, 0:128] = rotated(qacc[:, 0:128] + bk[...].astype(F32), cs[...], sn[...]).astype(BF16)
     kv[own_kv, 128:256] = (qacc[:, 128:256] + bv[...].astype(F32)).astype(BF16)
-    g_q_w.step(1)
+    g_q_w.step(2)
     g_kv.own()
-    g_q_w.step(2)
     g_q_w.crossed(1)
     g_kv.cross()
     g_q_w.step3()
     g_q_w.crossed(2)
     g_kv.step(1)
     g_q_w.step4()
-    g_q_w.crossed(3)
     g_kv.step(2)
     g_kv.crossed(1)
-    g_q_w.last()
-    tail(g_kv)
+    g_q_w.crossed(3)
     copies[4].wait()
     g_o_w.own()
+    g_q_w.last()
+    g_kv.step3()
+    g_kv.crossed(2)
     g_q_w.finish()
     project(wq, 512)
     for j in range(4):
         cols = pl.ds(j * HEAD_DIM, HEAD_DIM)
         value = qacc[:, cols] + bq[:, cols].astype(F32)
         qs[pl.ds(j * ROWS, ROWS), :] = rotated(value, cs[...], sn[...]).astype(BF16)
+    g_kv.step4()
+    g_kv.crossed(3)
+    g_kv.last()
+    g_o_w.cross()
     g_kv.finish()
-    g_o_w.cross()
 
     last_block = lax.div(s, 4)
+    score_bufs = (scores0, scores1)
+
+    def set_scores(j, block):
+        keys = kv[pl.ds(pl.multiple_of(block * KBLOCK, KBLOCK), KBLOCK), 0:128]
+        score_bufs[j % 2][...] = lax.dot_general(
+            qs[pl.ds(j * ROWS, ROWS), :], keys, (((1,), (1,)), ((), ())), preferred_element_type=F32
+        )
+
+    def attend(block, following, diagonal):
+        values = kv[pl.ds(pl.multiple_of(block * KBLOCK, KBLOCK), KBLOCK), 128:256]
+        weights = jnp.concatenate([values, jnp.ones((KBLOCK, HEAD_DIM), BF16)], axis=1)
+        for j in range(4):
+            rows = pl.ds(j * ROWS, ROWS)
+            set_scores((j + 1) % 4, block if j < 3 else following)
+            scores = score_bufs[j % 2][...]
+            if diagonal:
+                query_pos = s * ROWS + lax.broadcasted_iota(jnp.int32, (ROWS, KBLOCK), 0)
+                key_pos = block * KBLOCK + lax.broadcasted_iota(jnp.int32, (ROWS, KBLOCK), 1)
+                scores = jnp.where(query_pos >= key_pos, scores, -jnp.inf)
+            new_high = jnp.broadcast_to(jnp.max(scores, axis=-1, keepdims=True), (ROWS, HEAD_DIM))
+            if not diagonal:
+                old_high = high[rows, :]
+                new_high = jnp.maximum(old_high, new_high)
+            probs = jnp.exp2((scores - jnp.tile(new_high, (1, KBLOCK // HEAD_DIM))) * SCALE2)
+            mixed = jnp.dot(probs.astype(BF16), weights, preferred_element_type=F32)
+            if not diagonal:
+                fade = jnp.exp2((old_high - new_high) * SCALE2)
+                mixed = acc[rows, :] * jnp.tile(fade, (1, 2)) + mixed
+            acc[rows, :] = mixed
+            high[rows, :] = new_high
+
+    set_scores(0, last_block)
+    attend(last_block, 0, True)
+    relays = (
+        lambda: g_o_w.step_a(1),
+        lambda: g_o_w.step_b(1),
+        lambda: g_o_w.step_c(1),
+        lambda: g_o_w.step_a(2),
+        lambda: g_o_w.step_b(2),
+        lambda: g_o_w.step_c(2),
+        lambda: g_o_w.crossed(1),
+    )
+
+    @pl.loop(0, 7)
+    def _(block):
+        @pl.when(block < last_block)
+        def _():
+            attend(block, block + 1, False)
+
+        for k, relay in enumerate(relays):
+            pl.when(block == k)(relay)
+
     att32[...] = jnp.zeros(att32.shape, F32)
-
-    @pl.loop(0, 4)
-    def _(j):
-        query = qs[pl.ds(pl.multiple_of(j * ROWS, 16), ROWS), :]
-
-        def scores_of(block):
-            keys = kv[pl.ds(pl.multiple_of(block * KBLOCK, KBLOCK), KBLOCK), 0:128]
-            return lax.dot_general(query, keys, (((1,), (1,)), ((), ())), preferred_element_type=F32)
-
-        def mixed(probs, block):
-            values = kv[pl.ds(pl.multiple_of(block * KBLOCK, KBLOCK), KBLOCK), 128:256]
-            return jnp.dot(probs.astype(BF16), values, preferred_element_type=F32)
-
-        scores = scores_of(last_block)
-        query_pos = s * ROWS + lax.broadcasted_iota(jnp.int32, (ROWS, KBLOCK), 0)
-        key_pos = last_block * KBLOCK + lax.broadcasted_iota(jnp.int32, (ROWS, KBLOCK), 1)
-        scores = jnp.where(query_pos >= key_pos, scores, -jnp.inf)
-        highest = jnp.max(scores, axis=-1, keepdims=True)
-        probs = jnp.exp2((scores - highest) * SCALE2)
-        total = jnp.sum(probs, axis=-1, keepdims=True)
-        summed = mixed(probs, last_block)
-
-        def update(block, state):
-            highest, total, summed = state
-            scores = scores_of(block)
-            new_high = jnp.maximum(highest, jnp.max(scores, axis=-1, keepdims=True))
-            probs = jnp.exp2((scores - new_high) * SCALE2)
-            fade = jnp.exp2((highest - new_high) * SCALE2)
-            total = total * fade + jnp.sum(probs, axis=-1, keepdims=True)
-            return new_high, total, summed * fade + mixed(probs, block)
-
-        highest, total, summed = lax.fori_loop(0, last_block, update, (highest, total, summed))
-        tmp[...] = summed / total
-        cols = pl.ds(pl.multiple_of(j * HEAD_DIM, HEAD_DIM), HEAD_DIM)
+    for j in range(4):
+        rows = pl.ds(j * ROWS, ROWS)
+        tmp[...] = acc[rows, 0:HEAD_DIM] / acc[rows, HEAD_DIM : 2 * HEAD_DIM]
         for h in range(8):
             spot = PADROWS * (h % YS) + OWN * (h // YS)
-            att32[pl.ds(spot, OWN), cols] = tmp[pl.ds(h * OWN, OWN), :]
-
-        @pl.when(j < 2)
-        def _():
-            g_o_w.step(j + 1)
-
-        @pl.when(j == 2)
-        def _():
-            g_o_w.crossed(1)
-            g_o_w.step3()
-
-        @pl.when(j == 3)
-        def _():
-            g_o_w.crossed(2)
-            g_o_w.step4()
-
+            att32[pl.ds(spot, OWN), pl.ds(j * HEAD_DIM, HEAD_DIM)] = tmp[pl.ds(h * OWN, OWN), :]
     att[...] = att32[...].astype(BF16)
-    g_o_w.crossed(3)
-    g_o_w.last()
-    g_o_w.finish()
 
     y2 = wrap(y + 2, YS)
     y_next = wrap(y + 1, YS)
     y_prev = wrap(y - 1, YS)
-    half_cols = GCOLS // 2
 
     def move(src, dst, kind, g, dev):
         return pltpu.make_async_remote_copy(
@@ -320,23 +330,35 @@
         )
 
     def first(g, kind):
-        cols = pl.ds(g * GCOLS + kind * half_cols, half_cols)
-        return move(terms.at[y2, :, cols], r1.at[kind, g], kind, g, ym if kind else yp)
+        half = COLS[g] // 2
+        cols = pl.ds(BASE[g] + kind * half, half)
+        near = r1.at[kind, :, pl.ds(BASE[g] // 2, half)]
+        return move(terms.at[y2, :, cols], near, kind, g, ym if kind else yp)
 
     def second(g, kind):
-        cols = pl.ds(g * GCOLS, GCOLS)
+        cols = pl.ds(BASE[g], COLS[g])
         row = y_prev if kind else y_next
-        return move(terms.at[row, :, cols], r2.at[kind, g], 2 + kind, g, ym if kind else yp)
+        return move(terms.at[row, :, cols], r2.at[kind, :, cols], 2 + kind, g, ym if kind else yp)
 
     def third(g):
-        return move(xs.at[g], xr.at[g], 4, g, xhp)
+        cols = pl.ds(BASE[g], COLS[g])
+        return move(xs.at[:, cols], xr.at[:, cols], 4, g, xhp)
+
+    def slot_of(g, i):
+        ends = g in (0, 4)
+        other = lax.div(i, 2 if ends else 4)
+        side = 0 if ends else lax.rem(lax.div(i, 2), 2)
+        core = lax.rem(i, 2)
+        xx = x + other - 2 * x * other
+        return (xx * ZS + wrap(z + g - 2 * g * side, ZS)) * 2 + c + core - 2 * c * core
 
     def compute(g):
-        @pl.loop(0, GCOLS // 256)
+        g_o_w.sibling(g)
+
+        @pl.loop(0, COLS[g] // 256)
         def _(i):
-            slot = g * (GCOLS // 256) + i
-            depth = pl.ds(pl.multiple_of(slot * 512, 512), 512)
-            cols = pl.ds(pl.multiple_of(slot * 256, 256), 256)
+            depth = pl.ds(pl.multiple_of(slot_of(g, i) * 512, 512), 512)
+            cols = pl.ds(pl.multiple_of(BASE[g] + i * 256, 256), 256)
             term = jnp.dot(att[...], wo[depth, :], preferred_element_type=F32).astype(BF16)
             for k in range(YS):
                 terms[k, :, cols] = term[PADROWS * k : PADROWS * k + 2 * OWN]
@@ -348,29 +370,58 @@
         for kind in (0, 1):
             first(g, kind).wait_recv()
             row = y_prev if kind else y_next
-            cols = pl.ds(g * GCOLS + kind * half_cols, half_cols)
-            terms[row, :, cols] = (terms[row, :, cols].astype(F32) + r1[kind, g].astype(F32)).astype(BF16)
+            half = COLS[g] // 2
+            cols = pl.ds(BASE[g] + kind * half, half)
+            near = r1[kind, :, pl.ds(BASE[g] // 2, half)].astype(F32)
+            terms[row, :, cols] = (terms[row, :, cols].astype(F32) + near).astype(BF16)
             second(g, kind).start()
 
     def across(g):
         second(g, 0).wait_recv()
         second(g, 1).wait_recv()
-        cols = pl.ds(g * GCOLS, GCOLS)
-        tot[...] = terms[y, :, cols].astype(F32) + r2[0, g].astype(F32) + r2[1, g].astype(F32)
-        low, high = tot[0:OWN, :], tot[OWN : 2 * OWN, :]
+        cols = pl.ds(BASE[g], COLS[g])
+        part = tot.at[:, pl.ds(0, COLS[g])]
+        part[...] = terms[y, :, cols].astype(F32) + r2[0, :, cols].astype(F32) + r2[1, :, cols].astype(F32)
+        low, high_rows = part[0:OWN, :], part[OWN : 2 * OWN, :]
         lower = xh == 0
-        xs[g] = jnp.where(lower, high, low).astype(BF16)
-        keep[g] = jnp.where(lower, low, high)
+        xs[:, cols] = jnp.where(lower, high_rows, low).astype(BF16)
+        keep[:, cols] = jnp.where(lower, low, high_rows)
         third(g).start()
 
     def done(g):
         third(g).wait_recv()
-        out[:, pl.ds(g * GCOLS, GCOLS)] = (keep[g] + xr[g].astype(F32)).astype(BF16)
-
-    for t in range(GROUPS + 3):
-        for lag, stage in enumerate((compute, pair, across, done)):
-            if 0 <= t - lag < GROUPS:
-                stage(t - lag)
+
+        @pl.loop(0, COLS[g] // 256)
+        def _(i):
+            cols = pl.ds(pl.multiple_of(BASE[g] + i * 256, 256), 256)
+            there = pl.ds(pl.multiple_of(slot_of(g, i) * 256, 256), 256)
+            out[:, there] = (keep[:, cols] + xr[:, cols].astype(F32)).astype(BF16)
+
+    compute(0)
+    compute(1)
+    pair(0)
+    g_o_w.step3()
+    g_o_w.crossed(2)
+    compute(2)
+    pair(1)
+    across(0)
+    g_o_w.step4()
+    g_o_w.crossed(3)
+    compute(3)
+    pair(2)
+    g_o_w.last()
+    compute(4)
+    across(1)
+    done(0)
+    pair(3)
+    pair(4)
+    across(2)
+    done(1)
+    across(3)
+    across(4)
+    done(2)
+    done(3)
+    done(4)
 
     for g in range(GROUPS):
         for kind in (0, 1):
@@ -411,15 +462,19 @@
             pltpu.VMEM((YS * PADROWS, 512), F32),
             pltpu.VMEM((YS * PADROWS, 512), BF16),
             pltpu.VMEM((YS, 2 * OWN, D), BF16),
-            pltpu.VMEM((2, GROUPS, 2 * OWN, GCOLS // 2), BF16),
-            pltpu.VMEM((2, GROUPS, 2 * OWN, GCOLS), BF16),
-            pltpu.VMEM((GROUPS, OWN, GCOLS), BF16),
-            pltpu.VMEM((GROUPS, OWN, GCOLS), BF16),
-            pltpu.VMEM((2 * OWN, GCOLS), F32),
-            pltpu.VMEM((GROUPS, OWN, GCOLS), F32),
+            pltpu.VMEM((2, 2 * OWN, D // 2), BF16),
+            pltpu.VMEM((2, 2 * OWN, D), BF16),
+            pltpu.VMEM((OWN, D), BF16),
+            pltpu.VMEM((OWN, D), BF16),
+            pltpu.VMEM((2 * OWN, 2048), F32),
+            pltpu.VMEM((OWN, D), F32),
+            pltpu.VMEM((ROWS, KBLOCK), F32),
+            pltpu.VMEM((ROWS, KBLOCK), F32),
+            pltpu.VMEM((4 * ROWS, HEAD_DIM), F32),
+            pltpu.VMEM((4 * ROWS, 2 * HEAD_DIM), F32),
             dma((5,)),
             dma((4, 16, 2)),
-            dma((4,)),
+            dma((4, 5)),
             dma((4,)),
             dma((5, GROUPS)),
             dma((5, GROUPS)),

time: 191 us -> 168 us (0.88)
  Pallas kernels: 185 us -> 161 us
    pallas_call x1, Pallas kernels: 185 us -> 161 us  [local(): pl.pallas_call(kernel, name='layer', out_shape=jax.ShapeDtypeStruct((OWN,...]
where the time goes in v2:
time: 168 us; the launch traced here: 167 us
  Pallas kernels  161 us (96%)
  local copies, waits for them, and re-layouts  4.57 us (3%)
    pallas_call x1, Pallas kernels, local(): pl.pallas_call(kernel, name='layer', out_shape=jax.ShapeDtypeStruct((OWN,...  161 us

profile of v2, /device:TPU:1, one launch (start us, length us, event | category | flops | bytes accessed | tf_op | source)
XLA Modules:
  0.0 167.3 jit_solution(13123701682637846266)
XLA Ops:
  0.0 1.3 reshape.23.bq
  1.3 1.3 reshape.22.gain
  2.6 0.6 fusion
  3.2 0.8 pad_maximum_fusion
  4.1 161.3 %layer.1 = bf16[36,8192]{1,0:T(8,128)(2,1)} custom-call(bf16[288,8192]{1,0:T(8,128)(2,1)} %hidden.1, bf16[1,8192]{1,0:T(2,128)(2,1)} %reshape.22.gain, bf16[256,512]{1,0:T(8,128)(2,1)} %wq_in.1, bf16[256,128]{1,0:T(8,128)(2,1)} %wk_in.1, bf16[256,128]{1,0:T(8,128)(2,1)} %wv_in.1, bf16[1,512]{1,0:T(2,128)(2,1)} %reshape.23.bq, bf16[1,128]{1,0:T(2,128)(2,1)} %bitcast.2, ...), custom_call_target="tpu_custom_call" | custom-call | tf_op jit(solution)/shard_map/layer/pallas_call | solution.py:447
  165.4 2.0 %copy.11 = bf16[36,8192]{1,0:T(8,128)(2,1)} copy(bf16[36,8192]{1,0:T(8,128)(2,1)} %layer.1) | data formatting | bytes 1179648
  (2 shorter events, 0.0 us)

commit v3 on v2

--- a/solution.py
+++ b/solution.py
@@ -2,6 +2,7 @@
 
 import jax
 import jax.numpy as jnp
+import numpy as np
 from jax import lax
 from jax.experimental import pallas as pl
 from jax.experimental.pallas import tpu as pltpu
@@ -24,6 +25,103 @@
 BASE = (0, 1024, 3072, 5120, 7168)
 KBLOCK = 1152
 PADROWS = 80
+BEFORE = (
+    ("own", "k"),
+    ("own", "q"),
+    ("norm", 0),
+    ("cross", "k"),
+    ("a", "k", 1),
+    ("norm", 1),
+    ("b", "k", 1),
+    ("c", "k", 1),
+    ("norm", 2),
+    ("a", "k", 2),
+    ("norm", 3),
+    ("b", "k", 2),
+    ("c", "k", 2),
+    ("norm", 4),
+    ("cross", "q"),
+    ("x", "k", 1),
+    ("a", "q", 1),
+    ("s3", "k"),
+    ("norm", 5),
+    ("pk", 0),
+    ("b", "q", 1),
+    ("c", "q", 1),
+    ("x", "k", 2),
+    ("s4", "k"),
+    ("a", "q", 2),
+    ("x", "k", 3),
+    ("pk", 1),
+    ("pk", 2),
+    ("b", "q", 2),
+    ("last", "k"),
+    ("c", "q", 2),
+    ("pk", 3),
+    ("pk", 4),
+    ("ropek",),
+    ("own", "v"),
+    ("x", "q", 1),
+    ("s3", "q"),
+    ("x", "q", 2),
+    ("pq", 0),
+    ("cross", "v"),
+    ("a", "v", 1),
+    ("pq", 1),
+    ("b", "v", 1),
+    ("pq", 2),
+    ("s4", "q"),
+    ("c", "v", 1),
+    ("a", "v", 2),
+    ("b", "v", 2),
+    ("c", "v", 2),
+    ("x", "q", 3),
+    ("last", "q"),
+    ("own", "o"),
+    ("x", "v", 1),
+    ("pq", 3),
+    ("s3", "v"),
+    ("pq", 4),
+    ("ropeq",),
+    ("x", "v", 2),
+)
+BETWEEN = (
+    (),
+    (("cross", "o"), ("a", "o", 1), ),
+    (("s4", "v"), ("x", "v", 3), ("b", "o", 1), ),
+    (("c", "o", 1), ),
+    (("last", "v"), ("a", "o", 2), ),
+    (("b", "o", 2), ),
+    (("c", "o", 2), ("x", "o", 1), ),
+)
+AFTER = (
+    ("fin",),
+    ("comp", 0),
+    ("comp", 1),
+    ("s3", "o"),
+    ("x", "o", 2),
+    ("pair", 0),
+    ("pair", 1),
+    ("s4", "o"),
+    ("comp", 2),
+    ("x", "o", 3),
+    ("comp", 3),
+    ("across", 0),
+    ("last", "o"),
+    ("comp", 4),
+    ("pair", 2),
+    ("across", 1),
+    ("pair", 3),
+    ("across", 2),
+    ("pair", 4),
+    ("done", 0),
+    ("done", 1),
+    ("across", 3),
+    ("across", 4),
+    ("done", 2),
+    ("done", 3),
+    ("done", 4),
+)
 SCALE2 = HEAD_DIM**-0.5 * 1.4426950408889634
 
 
@@ -58,72 +156,60 @@
     def sem(self, s, part):
         return self.recv.at[self.kind, lax.div(s, 2), part]
 
-    def send(self, k, s, part, *devs):
+    def send(self, k, other, s, part, *devs):
         for dev in devs:
             self.copy(s, part, dev, self.sem(s, part)).start()
-        self.copy(s, part, self.sib, self.sib_sem.at[self.kind, k]).start()
-
-    def relay(self, k, s, part, *devs):
+        self.copy(s, part, self.sib, self.sib_sem.at[self.kind, k + 5 * other]).start()
+
+    def relay(self, k, other, dz, part, *devs):
+        s = self.at(1 - self.x if other else self.x, dz)
         self.copy(s, part, self.sib, self.sem(s, part)).wait_recv()
-        self.send(k, s, part, *devs)
+        self.send(k, other, s, part, *devs)
 
     def own(self):
-        s = self.at(self.x, 0)
         for part in (0, 1):
-            self.send(0, s, part, self.zp, self.zm, self.xp)
+            self.send(0, 0, self.at(self.x, 0), part, self.zp, self.zm, self.xp)
 
     def cross(self):
-        s = self.at(1 - self.x, 0)
-        self.relay(0, s, 0, self.zp, self.zm)
-        self.relay(0, s, 1)
-
-    def step_a(self, k):
-        self.relay(k, self.at(self.x, -k), 0, self.zp)
-        self.relay(k, self.at(self.x, k), 0, self.zm)
-
-    def step_b(self, k):
-        self.relay(k, self.at(self.x, -k), 1, self.zp, self.xp)
-        self.relay(k, self.at(self.x, k), 1, self.zm, self.xp)
-
-    def step_c(self, k):
-        self.relay(k, self.at(1 - self.x, -k), 0, self.zp)
-        self.relay(k, self.at(1 - self.x, k), 0, self.zm)
-
-    def step(self, k):
-        self.step_a(k)
-        self.step_b(k)
-        self.step_c(k)
-
-    def crossed(self, k):
-        self.relay(k, self.at(1 - self.x, -k), 1)
-        self.relay(k, self.at(1 - self.x, k), 1)
-
-    def step3(self):
-        lo, hi = self.at(self.x, -3), self.at(self.x, 3)
-        self.relay(3, lo, 0, self.zp)
-        self.relay(3, hi, 1, self.zm, self.xp)
-        self.relay(3, lo, 1, self.xp)
-        self.relay(3, hi, 0)
-        self.relay(3, self.at(1 - self.x, -3), 0)
-        self.relay(3, self.at(1 - self.x, 3), 0)
-
-    def step4(self):
-        far = self.at(self.x, 4)
-        self.relay(4, far, 0, self.xp)
-        self.relay(4, far, 1, self.xp)
+        self.relay(0, 1, 0, 0, self.zp, self.zm)
+        self.relay(0, 1, 0, 1)
+
+    def a(self, k):
+        self.relay(k, 0, -k, 0, self.zp)
+        self.relay(k, 0, k, 0, self.zm)
+
+    def b(self, k):
+        self.relay(k, 0, -k, 1, self.zp, self.xp)
+        self.relay(k, 0, k, 1, self.zm, self.xp)
+
+    def c2(self, k):
+        self.relay(k, 1, -k, 0, self.zp)
+        self.relay(k, 1, k, 0, self.zm)
+
+    def x2(self, k):
+        self.relay(k, 1, -k, 1)
+        self.relay(k, 1, k, 1)
+
+    def s3(self):
+        self.relay(3, 0, -3, 0, self.zp)
+        self.relay(3, 0, 3, 1, self.zm, self.xp)
+        self.relay(3, 0, -3, 1, self.xp)
+        self.relay(3, 0, 3, 0)
+        self.relay(3, 1, -3, 0)
+        self.relay(3, 1, 3, 0)
+
+    def s4(self):
+        self.relay(4, 0, 4, 0, self.xp)
+        self.relay(4, 0, 4, 1, self.xp)
 
     def last(self):
-        far = self.at(1 - self.x, 4)
-        self.relay(4, far, 0)
-        self.relay(4, far, 1)
-
-    def sibling(self, k):
-        part = self.buf.at[pl.ds(0, (2 if k in (0, 4) else 4) * self.rows)]
-        pltpu.make_async_copy(part, part, self.sib_sem.at[self.kind, k]).wait()
-
-    def finish(self):
-        for k in range(5):
-            self.sibling(k)
+        self.relay(4, 1, 4, 0)
+        self.relay(4, 1, 4, 1)
+
+    def sibling(self, k, *others):
+        for other in others:
+            part = self.buf.at[pl.ds(0, (1 if k in (0, 4) else 2) * self.rows)]
+            pltpu.make_async_copy(part, part, self.sib_sem.at[self.kind, k + 5 * other]).wait()
 
     def drain(self):
         part = self.buf.at[pl.ds(0, 31 * self.rows)]
@@ -135,10 +221,9 @@
 
 
 def kernel(
-    hidden, gain, wq_in, wk_in, wv_in, bq, bk, bv, wo_in, cs, sn, out,
-    hid, wkv, wq, kv, wo, qacc, qs, tmp, att32, att, terms, r1, r2, xs, xr, tot, keep,
-    scores0, scores1, high, acc,
-    local, recv, sib_sem, send_sem, rsem, r_send,
+    hidden, vecs, wq_in, wk_in, wv_in, wo_in, table, out,
+    hid, wkv, wq, kv, wo, kacc, qacc, qs, cs, sn, tmp, att32, att, terms, r1, r2, xs, xr, tot, keep,
+    scores0, scores1, high, acc, local, recv, sib_sem, send_sem, rsem, r_send,
 ):
     s = lax.axis_index("seq")
     head = lax.axis_index("head")
@@ -178,80 +263,57 @@
     copies[1].wait()
     copies[2].wait()
     pl.semaphore_wait(barrier, 7)
-    g_kv_w.own()
-    g_q_w.own()
-
-    copies[3].wait()
-
-    @pl.loop(0, ROWS // 16)
-    def _(i):
-        rows = pl.ds(pl.multiple_of(i * 16, 16), 16)
-        squares = jnp.zeros((16, 1024), F32)
-        for j in range(8):
-            part = hid[rows, pl.ds(j * 1024, 1024)].astype(F32)
-            squares = squares + part * part
-        inverse = lax.rsqrt(jnp.sum(squares, axis=-1, keepdims=True) * (1.0 / D) + EPSILON)
-        for j in range(8):
-            cols = pl.ds(j * 1024, 1024)
-            part = hid[rows, cols].astype(F32)
-            hid[rows, cols] = (part * inverse * gain[:, cols].astype(F32)).astype(BF16)
-
-    def stages(g):
-        g.step3()
-        g.crossed(2)
-        g.step4()
-        g.crossed(3)
-        g.last()
-
-    g_kv_w.cross()
-    g_kv_w.step(1)
-    g_q_w.cross()
-    g_kv_w.step(2)
-    g_kv_w.crossed(1)
-    g_q_w.step(1)
-    stages(g_kv_w)
-    g_kv_w.finish()
-
-    def project(weights, cols):
-        acc = qacc.at[:, pl.ds(0, cols)]
-        acc[...] = jnp.zeros((ROWS, cols), F32)
-
-        @pl.loop(0, 4)
+    kinds = {"k": g_kv_w, "q": g_q_w, "v": g_kv, "o": g_o_w}
+
+    def norm(chunk):
+        if chunk == 0:
+            copies[3].wait()
+
+        @pl.loop(3 * chunk, 3 * chunk + 3)
         def _(i):
-            depth = pl.ds(pl.multiple_of(i * 2048, 2048), 2048)
-            acc[...] += jnp.dot(hid[:, depth], weights[depth, :], preferred_element_type=F32)
-
-    project(wkv, 256)
-    own_kv = pl.ds(pl.multiple_of(s * ROWS, 16), ROWS)
-    kv[own_kv, 0:128] = rotated(qacc[:, 0:128] + bk[...].astype(F32), cs[...], sn[...]).astype(BF16)
-    kv[own_kv, 128:256] = (qacc[:, 128:256] + bv[...].astype(F32)).astype(BF16)
-    g_q_w.step(2)
-    g_kv.own()
-    g_q_w.crossed(1)
-    g_kv.cross()
-    g_q_w.step3()
-    g_q_w.crossed(2)
-    g_kv.step(1)
-    g_q_w.step4()
-    g_kv.step(2)
-    g_kv.crossed(1)
-    g_q_w.crossed(3)
-    copies[4].wait()
-    g_o_w.own()
-    g_q_w.last()
-    g_kv.step3()
-    g_kv.crossed(2)
-    g_q_w.finish()
-    project(wq, 512)
-    for j in range(4):
-        cols = pl.ds(j * HEAD_DIM, HEAD_DIM)
-        value = qacc[:, cols] + bq[:, cols].astype(F32)
-        qs[pl.ds(j * ROWS, ROWS), :] = rotated(value, cs[...], sn[...]).astype(BF16)
-    g_kv.step4()
-    g_kv.crossed(3)
-    g_kv.last()
-    g_o_w.cross()
-    g_kv.finish()
+            rows = pl.ds(pl.multiple_of(i * 16, 16), 16)
+            squares = jnp.zeros((16, 1024), F32)
+            for j in range(8):
+                part = hid[rows, pl.ds(j * 1024, 1024)].astype(F32)
+                squares = squares + part * part
+            inverse = lax.rsqrt(jnp.sum(squares, axis=-1, keepdims=True) * (1.0 / D) + EPSILON)
+            for j in range(8):
+                cols = pl.ds(j * 1024, 1024)
+                part = hid[rows, cols].astype(F32)
+                hid[rows, cols] = (part * inverse * vecs[:, cols]).astype(BF16)
+
+    def tables():
+        cos_row, sin_row = table[0:ROWS, :], table[ROWS : 2 * ROWS, :]
+        cos_first = table[pl.ds(2 * ROWS + s, 1), :]
+        sin_first = table[pl.ds(2 * ROWS + SEQ + s, 1), :]
+        cs[...] = cos_first * cos_row - sin_first * sin_row
+        sine = sin_first * cos_row + cos_first * sin_row
+        lane = lax.broadcasted_iota(jnp.int32, (ROWS, HEAD_DIM), 1)
+        sn[...] = jnp.where(lane < HEAD_DIM // 2, -sine, sine)
+
+    def project(gather, sums, k):
+        gather.sibling(k, 0, 1)
+        total = None
+        for other in (0, 1):
+            for dz in (0,) if k == 0 else (4,) if k == 4 else (-k, k):
+                place = lax.div(gather.at(1 - x if other else x, dz), 2)
+                depth = pl.ds(pl.multiple_of(place * 512, 512), 512)
+                term = jnp.dot(hid[:, depth], gather.buf[depth, :], preferred_element_type=F32)
+                total = term if total is None else total + term
+        sums[...] = total if k == 0 else sums[...] + total
+
+    def store_kv():
+        own_kv = pl.ds(pl.multiple_of(s * ROWS, 16), ROWS)
+        bk = vecs[:, D + 512 : D + 640]
+        bv = vecs[:, D + 640 : D + 768]
+        kv[own_kv, 0:128] = rotated(kacc[:, 0:128] + bk, cs[...], sn[...]).astype(BF16)
+        kv[own_kv, 128:256] = (kacc[:, 128:256] + bv).astype(BF16)
+
+    def store_q():
+        for j in range(4):
+            cols = pl.ds(j * HEAD_DIM, HEAD_DIM)
+            value = qacc[:, cols] + vecs[:, pl.ds(D + j * HEAD_DIM, HEAD_DIM)]
+            qs[pl.ds(j * ROWS, ROWS), :] = rotated(value, cs[...], sn[...]).astype(BF16)
 
     last_block = lax.div(s, 4)
     score_bufs = (scores0, scores1)
@@ -285,35 +347,25 @@
             acc[rows, :] = mixed
             high[rows, :] = new_high
 
-    set_scores(0, last_block)
-    attend(last_block, 0, True)
-    relays = (
-        lambda: g_o_w.step_a(1),
-        lambda: g_o_w.step_b(1),
-        lambda: g_o_w.step_c(1),
-        lambda: g_o_w.step_a(2),
-        lambda: g_o_w.step_b(2),
-        lambda: g_o_w.step_c(2),
-        lambda: g_o_w.crossed(1),
-    )
-
-    @pl.loop(0, 7)
-    def _(block):
-        @pl.when(block < last_block)
-        def _():
-            attend(block, block + 1, False)
-
-        for k, relay in enumerate(relays):
-            pl.when(block == k)(relay)
-
-    att32[...] = jnp.zeros(att32.shape, F32)
-    for j in range(4):
-        rows = pl.ds(j * ROWS, ROWS)
-        tmp[...] = acc[rows, 0:HEAD_DIM] / acc[rows, HEAD_DIM : 2 * HEAD_DIM]
-        for h in range(8):
-            spot = PADROWS * (h % YS) + OWN * (h // YS)
-            att32[pl.ds(spot, OWN), pl.ds(j * HEAD_DIM, HEAD_DIM)] = tmp[pl.ds(h * OWN, OWN), :]
-    att[...] = att32[...].astype(BF16)
+    def block_at(i):
+        own = (i < 3) | (i == 6)
+        column = jnp.where(own, x, 1 - x)
+        step = jnp.where(i >= 6, 2, jnp.where(i < 3, jnp.where(i == 2, 1, -i), jnp.where(i == 5, 1, 3 - i)))
+        return 4 * column + lax.rem(lax.div(z, 2) + step + 4, 4)
+
+    def arrived(i):
+        for k, other in {0: ((0, 0), (1, 0), (2, 0), (3, 0)), 2: ((0, 1), (1, 1)), 3: ((2, 1), (3, 1)), 5: ((4, 0),), 6: ((4, 1),)}.get(i, ()):
+            g_kv.sibling(k, other)
+
+    def finish_attention():
+        att32[...] = jnp.zeros(att32.shape, F32)
+        for j in range(4):
+            rows = pl.ds(j * ROWS, ROWS)
+            tmp[...] = acc[rows, 0:HEAD_DIM] / acc[rows, HEAD_DIM : 2 * HEAD_DIM]
+            for h in range(8):
+                spot = PADROWS * (h % YS) + OWN * (h // YS)
+                att32[pl.ds(spot, OWN), pl.ds(j * HEAD_DIM, HEAD_DIM)] = tmp[pl.ds(h * OWN, OWN), :]
+        att[...] = att32[...].astype(BF16)
 
     y2 = wrap(y + 2, YS)
     y_next = wrap(y + 1, YS)
@@ -353,7 +405,7 @@
         return (xx * ZS + wrap(z + g - 2 * g * side, ZS)) * 2 + c + core - 2 * c * core
 
     def compute(g):
-        g_o_w.sibling(g)
+        g_o_w.sibling(g, 0, 1)
 
         @pl.loop(0, COLS[g] // 256)
         def _(i):
@@ -397,31 +449,62 @@
             there = pl.ds(pl.multiple_of(slot_of(g, i) * 256, 256), 256)
             out[:, there] = (keep[:, cols] + xr[:, cols].astype(F32)).astype(BF16)
 
-    compute(0)
-    compute(1)
-    pair(0)
-    g_o_w.step3()
-    g_o_w.crossed(2)
-    compute(2)
-    pair(1)
-    across(0)
-    g_o_w.step4()
-    g_o_w.crossed(3)
-    compute(3)
-    pair(2)
-    g_o_w.last()
-    compute(4)
-    across(1)
-    done(0)
-    pair(3)
-    pair(4)
-    across(2)
-    done(1)
-    across(3)
-    across(4)
-    done(2)
-    done(3)
-    done(4)
+    def run(op):
+        name, rest = op[0], op[1:]
+        if name in ("own", "cross", "s3", "s4", "last"):
+            if op == ("own", "o"):
+                copies[4].wait()
+            getattr(kinds[rest[0]], name)()
+        elif name in ("a", "b"):
+            getattr(kinds[rest[0]], name)(rest[1])
+        elif name in ("c", "x"):
+            getattr(kinds[rest[0]], name + "2")(rest[1])
+        elif name == "pk":
+            project(g_kv_w, kacc, rest[0])
+        elif name == "pq":
+            project(g_q_w, qacc, rest[0])
+        else:
+            simple[name](*rest)
+
+    simple = {
+        "norm": norm,
+        "ropek": store_kv,
+        "ropeq": store_q,
+        "fin": finish_attention,
+        "comp": compute,
+        "pair": pair,
+        "across": across,
+        "done": done,
+    }
+    tables()
+    for op in BEFORE:
+        run(op)
+    arrived(0)
+    set_scores(0, last_block)
+    attend(last_block, block_at(1), True)
+
+    @pl.loop(1, 8)
+    def _(i):
+        for n, ops in enumerate(BETWEEN):
+
+            @pl.when(i == n + 1)
+            def _():
+                for op in ops:
+                    run(op)
+                arrived(n + 1)
+
+        block, following = block_at(i), block_at(jnp.minimum(i + 1, 7))
+
+        @pl.when(block < last_block)
+        def _():
+            attend(block, following, False)
+
+        @pl.when(block >= last_block)
+        def _():
+            set_scores(0, following)
+
+    for op in AFTER:
+        run(op)
 
     for g in range(GROUPS):
         for kind in (0, 1):
@@ -432,15 +515,17 @@
         g.drain()
 
 
+def rotary_table():
+    half_dim = HEAD_DIM // 2
+    freq = ROPE_BASE ** (-2.0 * np.arange(half_dim) / HEAD_DIM)
+    rows = np.arange(ROWS)[:, None] * freq
+    firsts = ROWS * np.arange(SEQ)[:, None] * freq
+    parts = (np.cos(rows), np.sin(rows), np.cos(firsts), np.sin(firsts))
+    return np.tile(np.concatenate(parts, axis=0), (1, 2)).astype(np.float32)
+
+
 def local(hidden, norm_gain, w_query, w_key, w_value, bias_query, bias_key, bias_value, w_out):
-    first_row = lax.axis_index("seq") * ROWS
-    positions = first_row + jnp.arange(ROWS, dtype=jnp.int32)
-    half_dim = HEAD_DIM // 2
-    freq = ROPE_BASE ** (-2.0 * jnp.arange(half_dim, dtype=F32) / HEAD_DIM)
-    angles = positions.astype(F32)[:, None] * freq[None, :]
-    cosine, sine = jnp.cos(angles), jnp.sin(angles)
-    cs = jnp.concatenate([cosine, cosine], axis=-1)
-    sn = jnp.concatenate([-sine, sine], axis=-1)
+    vecs = jnp.concatenate([norm_gain, bias_query, bias_key, bias_value]).astype(F32)
     vmem = pl.BlockSpec(memory_space=pltpu.VMEM)
     hbm = pl.BlockSpec(memory_space=pl.ANY)
     dma = pltpu.SemaphoreType.DMA
@@ -448,7 +533,7 @@
         kernel,
         name="layer",
         out_shape=jax.ShapeDtypeStruct((OWN, D), BF16),
-        in_specs=[hbm, vmem, hbm, hbm, hbm, vmem, vmem, vmem, hbm, vmem, vmem],
+        in_specs=[hbm, vmem, hbm, hbm, hbm, hbm, vmem],
         out_specs=vmem,
         scratch_shapes=[
             pltpu.VMEM((ROWS, D), BF16),
@@ -456,8 +541,11 @@
             pltpu.VMEM((D, 512), BF16),
             pltpu.VMEM((SEQ * ROWS, 256), BF16),
             pltpu.VMEM((SEQ * 512, 256), BF16),
+            pltpu.VMEM((ROWS, 256), F32),
             pltpu.VMEM((ROWS, 512), F32),
             pltpu.VMEM((4 * ROWS, HEAD_DIM), BF16),
+            pltpu.VMEM((ROWS, HEAD_DIM), F32),
+            pltpu.VMEM((ROWS, HEAD_DIM), F32),
             pltpu.VMEM((ROWS, HEAD_DIM), F32),
             pltpu.VMEM((YS * PADROWS, 512), F32),
             pltpu.VMEM((YS * PADROWS, 512), BF16),
@@ -474,7 +562,7 @@
             pltpu.VMEM((4 * ROWS, 2 * HEAD_DIM), F32),
             dma((5,)),
             dma((4, 16, 2)),
-            dma((4, 5)),
+            dma((4,10)),
             dma((4,)),
             dma((5, GROUPS)),
             dma((5, GROUPS)),
@@ -482,10 +570,7 @@
         compiler_params=pltpu.CompilerParams(
             collective_id=0, has_side_effects=True, vmem_limit_bytes=66 * 1000 * 1000
         ),
-    )(
-        hidden, norm_gain.reshape(1, D), w_query, w_key, w_value, bias_query.reshape(1, 512),
-        bias_key.reshape(1, 128), bias_value.reshape(1, 128), w_out, cs, sn,
-    )
+    )(hidden, vecs.reshape(1, -1), w_query, w_key, w_value, w_out, jnp.asarray(rotary_table()))
 
 
 def solution(mesh):

time: 168 us -> 145 us (0.86)
  Pallas kernels: 161 us -> 139 us
    pallas_call x1, Pallas kernels: 161 us -> 139 us  [local(): pl.pallas_call(kernel, name='layer', out_shape=jax.ShapeDtypeStruct((OWN,...]
    reshape x2 -> x0, local copies, waits for them, and re-layouts: 2.61 us -> none  [the longest x1 1.35 us: local(): norm_gain.reshape(1, D)]
where the time goes in v3:
time: 145 us; the launch traced here: 143 us
  Pallas kernels  139 us (96%)
  local copies, waits for them, and re-layouts  3.38 us (2%)
    pallas_call x1, Pallas kernels, local(): pl.pallas_call(kernel, name='layer', out_shape=jax.ShapeDtypeStruct((OWN,...  139 us

profile of v3, /device:TPU:1, one launch (start us, length us, event | category | flops | bytes accessed | tf_op | source)
XLA Modules:
  0.0 143.3 jit_solution(825512969893448603)
XLA Ops:
  0.0 0.7 concatenate.19
  0.7 0.7 concatenate.18
  1.4 1.3 maximum_convert_fusion.vecs
  2.8 138.6 %layer.1 = bf16[36,8192]{1,0:T(8,128)(2,1)} custom-call(bf16[288,8192]{1,0:T(8,128)(2,1)} %hidden.1, f32[1,8960]{1,0:T(1,128)} %maximum_convert_fusion.vecs, bf16[256,512]{1,0:T(8,128)(2,1)} %wq_in.1, bf16[256,128]{1,0:T(8,128)(2,1)} %wk_in.1, bf16[256,128]{1,0:T(8,128)(2,1)} %wv_in.1, bf16[512,256]{1,0:T(8,128)(2,1)} %wo_in.1, f32[640,128]{1,0:T(8,128)} %constant.2.clone.table), custom_call_target="tpu_custom_call" | custom-call | tf_op jit(solution)/shard_map/layer/pallas_call | solution.py:532
  141.3 2.0 %copy.12 = bf16[36,8192]{1,0:T(8,128)(2,1)} copy(bf16[36,8192]{1,0:T(8,128)(2,1)} %layer.1) | data formatting | bytes 1179648

commit v4 on v3

--- a/solution.py
+++ b/solution.py
@@ -25,71 +25,72 @@
 BASE = (0, 1024, 3072, 5120, 7168)
 KBLOCK = 1152
 PADROWS = 80
+XBASE = {3: 0}
+XCOLS = 2048
 BEFORE = (
     ("own", "k"),
+    ("norm", 0),
     ("own", "q"),
-    ("norm", 0),
     ("cross", "k"),
+    ("norm", 1),
     ("a", "k", 1),
-    ("norm", 1),
     ("b", "k", 1),
     ("c", "k", 1),
     ("norm", 2),
     ("a", "k", 2),
     ("norm", 3),
+    ("norm", 4),
     ("b", "k", 2),
     ("c", "k", 2),
-    ("norm", 4),
+    ("x", "k", 1),
     ("cross", "q"),
-    ("x", "k", 1),
+    ("norm", 5),
     ("a", "q", 1),
     ("s3", "k"),
-    ("norm", 5),
-    ("pk", 0),
     ("b", "q", 1),
     ("c", "q", 1),
     ("x", "k", 2),
+    ("pk", 0),
     ("s4", "k"),
+    ("x", "k", 3),
     ("a", "q", 2),
-    ("x", "k", 3),
+    ("b", "q", 2),
     ("pk", 1),
     ("pk", 2),
-    ("b", "q", 2),
     ("last", "k"),
-    ("c", "q", 2),
     ("pk", 3),
     ("pk", 4),
     ("ropek",),
+    ("pq", 0),
+    ("c", "q", 2),
     ("own", "v"),
     ("x", "q", 1),
     ("s3", "q"),
+    ("cross", "v"),
+    ("pq", 1),
     ("x", "q", 2),
-    ("pq", 0),
-    ("cross", "v"),
     ("a", "v", 1),
-    ("pq", 1),
     ("b", "v", 1),
-    ("pq", 2),
     ("s4", "q"),
     ("c", "v", 1),
+    ("pq", 2),
     ("a", "v", 2),
+    ("x", "q", 3),
     ("b", "v", 2),
     ("c", "v", 2),
-    ("x", "q", 3),
+    ("pq", 3),
+    ("x", "v", 1),
     ("last", "q"),
     ("own", "o"),
-    ("x", "v", 1),
-    ("pq", 3),
     ("s3", "v"),
     ("pq", 4),
     ("ropeq",),
-    ("x", "v", 2),
 )
 BETWEEN = (
     (),
     (("cross", "o"), ("a", "o", 1), ),
-    (("s4", "v"), ("x", "v", 3), ("b", "o", 1), ),
-    (("c", "o", 1), ),
+    (("x", "v", 2), ("s4", "v"), ("x", "v", 3), ("b", "o", 1), ("c", "o", 1), ),
+    (),
     (("last", "v"), ("a", "o", 2), ),
     (("b", "o", 2), ),
     (("c", "o", 2), ("x", "o", 1), ),
@@ -101,8 +102,8 @@
     ("s3", "o"),
     ("x", "o", 2),
     ("pair", 0),
+    ("s4", "o"),
     ("pair", 1),
-    ("s4", "o"),
     ("comp", 2),
     ("x", "o", 3),
     ("comp", 3),
@@ -111,12 +112,12 @@
     ("comp", 4),
     ("pair", 2),
     ("across", 1),
+    ("pair", 4),
     ("pair", 3),
     ("across", 2),
-    ("pair", 4),
+    ("across", 3),
+    ("done", 1),
     ("done", 0),
-    ("done", 1),
-    ("across", 3),
     ("across", 4),
     ("done", 2),
     ("done", 3),
@@ -221,9 +222,9 @@
 
 
 def kernel(
-    hidden, vecs, wq_in, wk_in, wv_in, wo_in, table, out,
+    hidden, gain_hbm, bq_hbm, bk_hbm, bv_hbm, wq_in, wk_in, wv_in, wo_in, table_hbm, out_hbm,
     hid, wkv, wq, kv, wo, kacc, qacc, qs, cs, sn, tmp, att32, att, terms, r1, r2, xs, xr, tot, keep,
-    scores0, scores1, high, acc, local, recv, sib_sem, send_sem, rsem, r_send,
+    scores0, scores1, high, acc, vecs, out, out_sem, att_rows, gain_in, bq_in, bk_in, bv_in, table, x_terms, x_recv, x_sum, x_wide, x_r1, x_r2, local, recv, sib_sem, send_sem, rsem, r_send,
 ):
     s = lax.axis_index("seq")
     head = lax.axis_index("head")
@@ -251,14 +252,19 @@
         pltpu.make_async_copy(wq_in, wq.at[mine], local.at[2]),
         pltpu.make_async_copy(hidden, hid, local.at[3]),
         pltpu.make_async_copy(wo_in, wo.at[mine_o], local.at[4]),
+        pltpu.make_async_copy(gain_hbm, gain_in, local.at[5]),
+        pltpu.make_async_copy(bq_hbm, bq_in, local.at[6]),
+        pltpu.make_async_copy(bk_hbm, bk_in, local.at[7]),
+        pltpu.make_async_copy(bv_hbm, bv_in, local.at[8]),
+        pltpu.make_async_copy(table_hbm, table, local.at[9]),
     ]
-    for copy in copies:
-        copy.start()
     barrier = pltpu.get_barrier_semaphore()
     for dev in (g_q_w.zp, g_q_w.zm, g_q_w.xp, g_q_w.sib):
         pl.semaphore_signal(barrier, inc=1, device_id=(dev, head), device_id_type=MESH)
     for dev in (yp, ym, xhp):
         pl.semaphore_signal(barrier, inc=1, device_id=(s, dev), device_id_type=MESH)
+    for copy in copies:
+        copy.start()
     copies[0].wait()
     copies[1].wait()
     copies[2].wait()
@@ -267,6 +273,7 @@
 
     def norm(chunk):
         if chunk == 0:
+            tables()
             copies[3].wait()
 
         @pl.loop(3 * chunk, 3 * chunk + 3)
@@ -283,6 +290,14 @@
                 hid[rows, cols] = (part * inverse * vecs[:, cols]).astype(BF16)
 
     def tables():
+        for copy in copies[5:]:
+            copy.wait()
+        for i in range(D // HEAD_DIM):
+            vecs[:, pl.ds(i * HEAD_DIM, HEAD_DIM)] = gain_in[pl.ds(i, 1), :].astype(F32)
+        for i in range(4):
+            vecs[:, pl.ds(D + i * HEAD_DIM, HEAD_DIM)] = bq_in[pl.ds(i, 1), :].astype(F32)
+        vecs[:, pl.ds(D + 512, HEAD_DIM)] = bk_in[...].astype(F32)
+        vecs[:, pl.ds(D + 640, HEAD_DIM)] = bv_in[...].astype(F32)
         cos_row, sin_row = table[0:ROWS, :], table[ROWS : 2 * ROWS, :]
         cos_first = table[pl.ds(2 * ROWS + s, 1), :]
         sin_first = table[pl.ds(2 * ROWS + SEQ + s, 1), :]
@@ -362,6 +377,7 @@
         for j in range(4):
             rows = pl.ds(j * ROWS, ROWS)
             tmp[...] = acc[rows, 0:HEAD_DIM] / acc[rows, HEAD_DIM : 2 * HEAD_DIM]
+            att_rows[:, pl.ds(j * HEAD_DIM, HEAD_DIM)] = tmp[...].astype(BF16)
             for h in range(8):
                 spot = PADROWS * (h % YS) + OWN * (h // YS)
                 att32[pl.ds(spot, OWN), pl.ds(j * HEAD_DIM, HEAD_DIM)] = tmp[pl.ds(h * OWN, OWN), :]
@@ -448,6 +464,68 @@
             cols = pl.ds(pl.multiple_of(BASE[g] + i * 256, 256), 256)
             there = pl.ds(pl.multiple_of(slot_of(g, i) * 256, 256), 256)
             out[:, there] = (keep[:, cols] + xr[:, cols].astype(F32)).astype(BF16)
+            pltpu.make_async_copy(out.at[:, there], out_hbm.at[:, there], out_sem).start()
+
+    def x_cols(g):
+        return pl.ds(XBASE[g], COLS[g])
+
+    def x_first(g):
+        return move(x_terms.at[1 - xh, :, x_cols(g)], x_recv.at[:, x_cols(g)], 4, g, xhp)
+
+    def x_second(g, kind):
+        half = COLS[g] // 2
+        near = x_r1.at[kind, :, pl.ds(XBASE[g] // 2, half)]
+        return move(x_sum.at[y2, :, pl.ds(XBASE[g] + kind * half, half)], near, kind, g, ym if kind else yp)
+
+    def x_third(g, kind):
+        row = y_prev if kind else y_next
+        return move(x_sum.at[row, :, x_cols(g)], x_r2.at[kind, :, x_cols(g)], 2 + kind, g, ym if kind else yp)
+
+    def x_compute(g):
+        g_o_w.sibling(g, 0, 1)
+
+        @pl.loop(0, COLS[g] // 256)
+        def _(i):
+            depth = pl.ds(pl.multiple_of(slot_of(g, i) * 512, 512), 512)
+            cols = pl.ds(pl.multiple_of(XBASE[g] + i * 256, 256), 256)
+            term = jnp.dot(att_rows[...], wo[depth, :], preferred_element_type=F32).astype(BF16)
+            for k in range(2):
+                x_terms[k, :, cols] = term[ROWS // 2 * k : ROWS // 2 * (k + 1)]
+
+        x_first(g).start()
+
+    def x_pair(g):
+        x_first(g).wait_recv()
+        wide = x_wide.at[:, pl.ds(0, COLS[g])]
+        wide[...] = x_terms[xh, :, x_cols(g)].astype(F32) + x_recv[:, x_cols(g)].astype(F32)
+        for k in range(YS):
+            x_sum[k, :, x_cols(g)] = wide[pl.ds(OWN * k, OWN), :].astype(BF16)
+        x_second(g, 0).start()
+        x_second(g, 1).start()
+
+    def x_across(g):
+        half = COLS[g] // 2
+        for kind in (0, 1):
+            x_second(g, kind).wait_recv()
+            row = y_prev if kind else y_next
+            cols = pl.ds(XBASE[g] + kind * half, half)
+            near = x_r1[kind, :, pl.ds(XBASE[g] // 2, half)].astype(F32)
+            x_sum[row, :, cols] = (x_sum[row, :, cols].astype(F32) + near).astype(BF16)
+            x_third(g, kind).start()
+
+    def x_done(g):
+        x_third(g, 0).wait_recv()
+        x_third(g, 1).wait_recv()
+
+        @pl.loop(0, COLS[g] // 256)
+        def _(i):
+            cols = pl.ds(pl.multiple_of(XBASE[g] + i * 256, 256), 256)
+            there = pl.ds(pl.multiple_of(slot_of(g, i) * 256, 256), 256)
+            value = x_sum[y, :, cols].astype(F32) + x_r2[0, :, cols].astype(F32)
+            out[:, there] = (value + x_r2[1, :, cols].astype(F32)).astype(BF16)
+            pltpu.make_async_copy(out.at[:, there], out_hbm.at[:, there], out_sem).start()
+
+    x_stages = {"comp": x_compute, "pair": x_pair, "across": x_across, "done": x_done}
 
     def run(op):
         name, rest = op[0], op[1:]
@@ -463,6 +541,8 @@
             project(g_kv_w, kacc, rest[0])
         elif name == "pq":
             project(g_q_w, qacc, rest[0])
+        elif name in x_stages and rest[0] in XBASE:
+            x_stages[name](rest[0])
         else:
             simple[name](*rest)
 
@@ -476,7 +556,6 @@
         "across": across,
         "done": done,
     }
-    tables()
     for op in BEFORE:
         run(op)
     arrived(0)
@@ -507,12 +586,14 @@
         run(op)
 
     for g in range(GROUPS):
+        one, two, three = (x_second, x_third, x_first) if g in XBASE else (first, second, third)
         for kind in (0, 1):
-            first(g, kind).wait_send()
-            second(g, kind).wait_send()
-        third(g).wait_send()
+            one(g, kind).wait_send()
+            two(g, kind).wait_send()
+        three(g).wait_send()
     for g in (g_kv_w, g_q_w, g_kv, g_o_w):
         g.drain()
+    pltpu.make_async_copy(out, out_hbm, out_sem).wait()
 
 
 def rotary_table():
@@ -525,7 +606,6 @@
 
 
 def local(hidden, norm_gain, w_query, w_key, w_value, bias_query, bias_key, bias_value, w_out):
-    vecs = jnp.concatenate([norm_gain, bias_query, bias_key, bias_value]).astype(F32)
     vmem = pl.BlockSpec(memory_space=pltpu.VMEM)
     hbm = pl.BlockSpec(memory_space=pl.ANY)
     dma = pltpu.SemaphoreType.DMA
@@ -533,8 +613,8 @@
         kernel,
         name="layer",
         out_shape=jax.ShapeDtypeStruct((OWN, D), BF16),
-        in_specs=[hbm, vmem, hbm, hbm, hbm, hbm, vmem],
-        out_specs=vmem,
+        in_specs=[hbm] * 10,
+        out_specs=hbm,
         scratch_shapes=[
             pltpu.VMEM((ROWS, D), BF16),
             pltpu.VMEM((D, 256), BF16),
@@ -560,7 +640,22 @@
             pltpu.VMEM((ROWS, KBLOCK), F32),
             pltpu.VMEM((4 * ROWS, HEAD_DIM), F32),
             pltpu.VMEM((4 * ROWS, 2 * HEAD_DIM), F32),
-            dma((5,)),
+            pltpu.VMEM((1, D + 768), F32),
+            pltpu.VMEM((OWN, D), BF16),
+            dma,
+            pltpu.VMEM((ROWS, 512), BF16),
+            pltpu.VMEM((D // HEAD_DIM, HEAD_DIM), BF16),
+            pltpu.VMEM((4, HEAD_DIM), BF16),
+            pltpu.VMEM((1, HEAD_DIM), BF16),
+            pltpu.VMEM((1, HEAD_DIM), BF16),
+            pltpu.VMEM((2 * ROWS + 2 * SEQ, HEAD_DIM), F32),
+            pltpu.VMEM((2, ROWS // 2, XCOLS), BF16),
+            pltpu.VMEM((ROWS // 2, XCOLS), BF16),
+            pltpu.VMEM((YS, OWN, XCOLS), BF16),
+            pltpu.VMEM((ROWS // 2, 2048), F32),
+            pltpu.VMEM((2, OWN, XCOLS // 2), BF16),
+            pltpu.VMEM((2, OWN, XCOLS), BF16),
+            dma((10,)),
             dma((4, 16, 2)),
             dma((4,10)),
             dma((4,)),
@@ -570,7 +665,11 @@
         compiler_params=pltpu.CompilerParams(
             collective_id=0, has_side_effects=True, vmem_limit_bytes=66 * 1000 * 1000
         ),
-    )(hidden, vecs.reshape(1, -1), w_query, w_key, w_value, w_out, jnp.asarray(rotary_table()))
+    )(
+        hidden, norm_gain.reshape(-1, HEAD_DIM), bias_query.reshape(-1, HEAD_DIM),
+        bias_key.reshape(-1, HEAD_DIM), bias_value.reshape(-1, HEAD_DIM),
+        w_query, w_key, w_value, w_out, jnp.asarray(rotary_table()),
+    )
 
 
 def solution(mesh):

time: 145 us -> 136 us (0.938)
  Pallas kernels: 139 us -> 134 us
    pallas_call x1, Pallas kernels: 139 us -> 134 us  [local(): pl.pallas_call(kernel, name='layer', out_shape=jax.ShapeDtypeStruct((OWN,...]
where the time goes in v4:
time: 136 us
  Pallas kernels  134 us (99%)
  local copies, waits for them, and re-layouts  1.97 us (1%)
    pallas_call x1, Pallas kernels, local(): pl.pallas_call(kernel, name='layer', out_shape=jax.ShapeDtypeStruct((OWN,...  134 us

profile of v4, /device:TPU:1, one launch (start us, length us, event | category | flops | bytes accessed | tf_op | source)
XLA Modules:
  0.0 135.5 jit_solution(6097196394689535097)
XLA Ops:
  0.0 133.5 %layer.1 = bf16[36,8192]{1,0:T(8,128)(2,1)} custom-call(bf16[288,8192]{1,0:T(8,128)(2,1)} %hidden.1, bf16[64,128]{1,0:T(8,128)(2,1)} %bitcast.4, bf16[4,128]{1,0:T(4,128)(2,1)} %bitcast.5, bf16[1,128]{1,0:T(2,128)(2,1)} %bitcast.6, bf16[1,128]{1,0:T(2,128)(2,1)} %bitcast.7, bf16[256,512]{1,0:T(8,128)(2,1)} %wq_in.1, bf16[256,128]{1,0:T(8,128)(2,1)} %wk_in.1, ...), custom_call_target="tpu_custom_call" | custom-call | tf_op jit(solution)/shard_map/layer/pallas_call | solution.py:612
  133.5 2.0 %copy.12 = bf16[36,8192]{1,0:T(8,128)(2,1)} copy(bf16[36,8192]{1,0:T(8,128)(2,1)} %layer.1) | data formatting | bytes 1179648

commit v5 on v4

--- a/solution.py
+++ b/solution.py
@@ -20,12 +20,13 @@
 ROWS = 288
 D = 8192
 OWN = 36
-GROUPS = 5
-COLS = (1024, 2048, 2048, 2048, 1024)
-BASE = (0, 1024, 3072, 5120, 7168)
+GROUPS = 8
+DISTANCE = (0, 1, 1, 2, 2, 3, 3, 4)
+COLS = (1024,) * GROUPS
+BASE = tuple(1024 * g for g in range(GROUPS))
 KBLOCK = 1152
 PADROWS = 80
-XBASE = {3: 0}
+XBASE = {5: 0, 6: 1024}
 XCOLS = 2048
 BEFORE = (
     ("own", "k"),
@@ -99,29 +100,41 @@
     ("fin",),
     ("comp", 0),
     ("comp", 1),
+    ("comp", 2),
     ("s3", "o"),
     ("x", "o", 2),
     ("pair", 0),
     ("s4", "o"),
     ("pair", 1),
-    ("comp", 2),
+    ("pair", 2),
+    ("comp", 3),
+    ("comp", 4),
     ("x", "o", 3),
-    ("comp", 3),
+    ("comp", 5),
+    ("comp", 6),
     ("across", 0),
     ("last", "o"),
-    ("comp", 4),
-    ("pair", 2),
+    ("comp", 7),
+    ("pair", 3),
+    ("pair", 4),
     ("across", 1),
-    ("pair", 4),
-    ("pair", 3),
     ("across", 2),
+    ("pair", 7),
+    ("pair", 5),
+    ("pair", 6),
     ("across", 3),
+    ("across", 4),
+    ("across", 5),
+    ("across", 6),
     ("done", 1),
+    ("done", 2),
     ("done", 0),
-    ("across", 4),
-    ("done", 2),
+    ("across", 7),
     ("done", 3),
     ("done", 4),
+    ("done", 5),
+    ("done", 6),
+    ("done", 7),
 )
 SCALE2 = HEAD_DIM**-0.5 * 1.4426950408889634
 
@@ -341,7 +354,6 @@
 
     def attend(block, following, diagonal):
         values = kv[pl.ds(pl.multiple_of(block * KBLOCK, KBLOCK), KBLOCK), 128:256]
-        weights = jnp.concatenate([values, jnp.ones((KBLOCK, HEAD_DIM), BF16)], axis=1)
         for j in range(4):
             rows = pl.ds(j * ROWS, ROWS)
             set_scores((j + 1) % 4, block if j < 3 else following)
@@ -355,11 +367,16 @@
                 old_high = high[rows, :]
                 new_high = jnp.maximum(old_high, new_high)
             probs = jnp.exp2((scores - jnp.tile(new_high, (1, KBLOCK // HEAD_DIM))) * SCALE2)
-            mixed = jnp.dot(probs.astype(BF16), weights, preferred_element_type=F32)
+            part = probs[:, 0:HEAD_DIM]
+            for n in range(1, KBLOCK // HEAD_DIM):
+                part = part + probs[:, n * HEAD_DIM : (n + 1) * HEAD_DIM]
+            mixed = jnp.dot(probs.astype(BF16), values, preferred_element_type=F32)
             if not diagonal:
                 fade = jnp.exp2((old_high - new_high) * SCALE2)
-                mixed = acc[rows, :] * jnp.tile(fade, (1, 2)) + mixed
-            acc[rows, :] = mixed
+                mixed = acc[rows, 0:HEAD_DIM] * fade + mixed
+                part = acc[rows, HEAD_DIM : 2 * HEAD_DIM] * fade + part
+            acc[rows, 0:HEAD_DIM] = mixed
+            acc[rows, HEAD_DIM : 2 * HEAD_DIM] = part
             high[rows, :] = new_high
 
     def block_at(i):
@@ -376,7 +393,9 @@
         att32[...] = jnp.zeros(att32.shape, F32)
         for j in range(4):
             rows = pl.ds(j * ROWS, ROWS)
-            tmp[...] = acc[rows, 0:HEAD_DIM] / acc[rows, HEAD_DIM : 2 * HEAD_DIM]
+            tmp[...] = acc[rows, 0:HEAD_DIM] / jnp.sum(
+                acc[rows, HEAD_DIM : 2 * HEAD_DIM], axis=-1, keepdims=True
+            )
             att_rows[:, pl.ds(j * HEAD_DIM, HEAD_DIM)] = tmp[...].astype(BF16)
             for h in range(8):
                 spot = PADROWS * (h % YS) + OWN * (h // YS)
@@ -413,15 +432,20 @@
         return move(xs.at[:, cols], xr.at[:, cols], 4, g, xhp)
 
     def slot_of(g, i):
-        ends = g in (0, 4)
-        other = lax.div(i, 2 if ends else 4)
-        side = 0 if ends else lax.rem(lax.div(i, 2), 2)
+        k = DISTANCE[g]
+        ends = k in (0, 4)
+        other = lax.div(i, 2) if ends else 1 - g % 2
+        side = 0 if ends else lax.div(i, 2)
         core = lax.rem(i, 2)
         xx = x + other - 2 * x * other
-        return (xx * ZS + wrap(z + g - 2 * g * side, ZS)) * 2 + c + core - 2 * c * core
+        return (xx * ZS + wrap(z + k - 2 * k * side, ZS)) * 2 + c + core - 2 * c * core
+
+    def shards_in(g):
+        k = DISTANCE[g]
+        g_o_w.sibling(k, *((0, 1) if k in (0, 4) else (1 - g % 2,)))
 
     def compute(g):
-        g_o_w.sibling(g, 0, 1)
+        shards_in(g)
 
         @pl.loop(0, COLS[g] // 256)
         def _(i):
@@ -482,7 +506,7 @@
         return move(x_sum.at[row, :, x_cols(g)], x_r2.at[kind, :, x_cols(g)], 2 + kind, g, ym if kind else yp)
 
     def x_compute(g):
-        g_o_w.sibling(g, 0, 1)
+        shards_in(g)
 
         @pl.loop(0, COLS[g] // 256)
         def _(i):
@@ -634,7 +658,7 @@
             pltpu.VMEM((2, 2 * OWN, D), BF16),
             pltpu.VMEM((OWN, D), BF16),
             pltpu.VMEM((OWN, D), BF16),
-            pltpu.VMEM((2 * OWN, 2048), F32),
+            pltpu.VMEM((2 * OWN, 1024), F32),
             pltpu.VMEM((OWN, D), F32),
             pltpu.VMEM((ROWS, KBLOCK), F32),
             pltpu.VMEM((ROWS, KBLOCK), F32),
@@ -652,7 +676,7 @@
             pltpu.VMEM((2, ROWS // 2, XCOLS), BF16),
             pltpu.VMEM((ROWS // 2, XCOLS), BF16),
             pltpu.VMEM((YS, OWN, XCOLS), BF16),
-            pltpu.VMEM((ROWS // 2, 2048), F32),
+            pltpu.VMEM((ROWS // 2, 1024), F32),
             pltpu.VMEM((2, OWN, XCOLS // 2), BF16),
             pltpu.VMEM((2, OWN, XCOLS), BF16),
             dma((10,)),

time: 136 us -> 134 us (0.985)
  Pallas kernels: 134 us -> 132 us
    pallas_call x1, Pallas kernels: 134 us -> 132 us  [local(): pl.pallas_call(kernel, name='layer', out_shape=jax.ShapeDtypeStruct((OWN,...]
where the time goes in v5:
time: 134 us
  Pallas kernels  132 us (99%)
  local copies, waits for them, and re-layouts  1.97 us (1%)
    pallas_call x1, Pallas kernels, local(): pl.pallas_call(kernel, name='layer', out_shape=jax.ShapeDtypeStruct((OWN,...  132 us

profile of v5, /device:TPU:1, one launch (start us, length us, event | category | flops | bytes accessed | tf_op | source)
XLA Modules:
  0.0 134.1 jit_solution(15918653281795791644)
XLA Ops:
  0.0 132.1 %layer.1 = bf16[36,8192]{1,0:T(8,128)(2,1)} custom-call(bf16[288,8192]{1,0:T(8,128)(2,1)} %hidden.1, bf16[64,128]{1,0:T(8,128)(2,1)} %bitcast.4, bf16[4,128]{1,0:T(4,128)(2,1)} %bitcast.5, bf16[1,128]{1,0:T(2,128)(2,1)} %bitcast.6, bf16[1,128]{1,0:T(2,128)(2,1)} %bitcast.7, bf16[256,512]{1,0:T(8,128)(2,1)} %wq_in.1, bf16[256,128]{1,0:T(8,128)(2,1)} %wk_in.1, ...), custom_call_target="tpu_custom_call" | custom-call | tf_op jit(solution)/shard_map/layer/pallas_call | solution.py:636
  132.1 2.0 %copy.12 = bf16[36,8192]{1,0:T(8,128)(2,1)} copy(bf16[36,8192]{1,0:T(8,128)(2,1)} %layer.1) | data formatting | bytes 1179648

commit v6 on v5

--- a/solution.py
+++ b/solution.py
@@ -26,113 +26,114 @@
 BASE = tuple(1024 * g for g in range(GROUPS))
 KBLOCK = 1152
 PADROWS = 80
-XBASE = {5: 0, 6: 1024}
+XBASE = {1: 0, 6: 1024}
 XCOLS = 2048
 BEFORE = (
     ("own", "k"),
-    ("norm", 0),
     ("own", "q"),
     ("cross", "k"),
+    ("norm", 0),
     ("norm", 1),
+    ("norm", 2),
     ("a", "k", 1),
     ("b", "k", 1),
     ("c", "k", 1),
-    ("norm", 2),
+    ("norm", 3),
     ("a", "k", 2),
-    ("norm", 3),
-    ("norm", 4),
     ("b", "k", 2),
     ("c", "k", 2),
     ("x", "k", 1),
     ("cross", "q"),
+    ("s3", "k"),
+    ("a", "q", 1),
+    ("x", "k", 2),
+    ("norm", 4),
     ("norm", 5),
-    ("a", "q", 1),
-    ("s3", "k"),
     ("b", "q", 1),
-    ("c", "q", 1),
-    ("x", "k", 2),
     ("pk", 0),
     ("s4", "k"),
+    ("c", "q", 1),
+    ("a", "q", 2),
     ("x", "k", 3),
-    ("a", "q", 2),
+    ("pk", 1),
     ("b", "q", 2),
-    ("pk", 1),
+    ("pq", 0),
+    ("last", "k"),
+    ("c", "q", 2),
     ("pk", 2),
-    ("last", "k"),
     ("pk", 3),
     ("pk", 4),
     ("ropek",),
-    ("pq", 0),
-    ("c", "q", 2),
+    ("x", "q", 1),
     ("own", "v"),
-    ("x", "q", 1),
     ("s3", "q"),
     ("cross", "v"),
-    ("pq", 1),
-    ("x", "q", 2),
     ("a", "v", 1),
     ("b", "v", 1),
+    ("x", "q", 2),
     ("s4", "q"),
     ("c", "v", 1),
-    ("pq", 2),
     ("a", "v", 2),
     ("x", "q", 3),
+    ("pq", 1),
     ("b", "v", 2),
     ("c", "v", 2),
+    ("pq", 2),
+    ("x", "v", 1),
+    ("own", "o"),
+    ("last", "q"),
     ("pq", 3),
-    ("x", "v", 1),
-    ("last", "q"),
-    ("own", "o"),
     ("s3", "v"),
     ("pq", 4),
     ("ropeq",),
+    ("x", "v", 2),
 )
 BETWEEN = (
     (),
     (("cross", "o"), ("a", "o", 1), ),
-    (("x", "v", 2), ("s4", "v"), ("x", "v", 3), ("b", "o", 1), ("c", "o", 1), ),
+    (("s4", "v"), ("x", "v", 3), ("b", "o", 1), ("c", "o", 1), ),
     (),
-    (("last", "v"), ("a", "o", 2), ),
-    (("b", "o", 2), ),
+    (("last", "v"), ),
+    (("a", "o", 2), ("b", "o", 2), ),
     (("c", "o", 2), ("x", "o", 1), ),
 )
 AFTER = (
     ("fin",),
+    ("comp", 1),
+    ("comp", 3),
     ("comp", 0),
-    ("comp", 1),
     ("comp", 2),
     ("s3", "o"),
     ("x", "o", 2),
+    ("pair", 3),
     ("pair", 0),
     ("s4", "o"),
+    ("comp", 5),
+    ("pair", 2),
+    ("x", "o", 3),
+    ("comp", 4),
+    ("across", 3),
+    ("pair", 5),
     ("pair", 1),
-    ("pair", 2),
-    ("comp", 3),
-    ("comp", 4),
-    ("x", "o", 3),
-    ("comp", 5),
     ("comp", 6),
-    ("across", 0),
     ("last", "o"),
     ("comp", 7),
-    ("pair", 3),
     ("pair", 4),
+    ("done", 3),
+    ("across", 5),
+    ("pair", 7),
+    ("across", 0),
+    ("pair", 6),
+    ("across", 2),
+    ("across", 4),
     ("across", 1),
-    ("across", 2),
-    ("pair", 7),
-    ("pair", 5),
-    ("pair", 6),
-    ("across", 3),
-    ("across", 4),
-    ("across", 5),
+    ("across", 7),
     ("across", 6),
+    ("done", 5),
+    ("done", 4),
+    ("done", 0),
+    ("done", 2),
     ("done", 1),
-    ("done", 2),
-    ("done", 0),
-    ("across", 7),
-    ("done", 3),
-    ("done", 4),
-    ("done", 5),
     ("done", 6),
     ("done", 7),
 )

time: 134 us -> 134 us (level)
  no operation moved by 1% of the time
where the time goes in v6:
time: 134 us; the launch traced here: 133 us
  Pallas kernels  132 us (99%)
  local copies, waits for them, and re-layouts  1.97 us (1%)
    pallas_call x1, Pallas kernels, local(): pl.pallas_call(kernel, name='layer', out_shape=jax.ShapeDtypeStruct((OWN,...  132 us

profile of v6, /device:TPU:1, one launch (start us, length us, event | category | flops | bytes accessed | tf_op | source)
XLA Modules:
  0.0 133.5 jit_solution(13140637030381778821)
XLA Ops:
  0.0 131.5 %layer.1 = bf16[36,8192]{1,0:T(8,128)(2,1)} custom-call(bf16[288,8192]{1,0:T(8,128)(2,1)} %hidden.1, bf16[64,128]{1,0:T(8,128)(2,1)} %bitcast.4, bf16[4,128]{1,0:T(4,128)(2,1)} %bitcast.5, bf16[1,128]{1,0:T(2,128)(2,1)} %bitcast.6, bf16[1,128]{1,0:T(2,128)(2,1)} %bitcast.7, bf16[256,512]{1,0:T(8,128)(2,1)} %wq_in.1, bf16[256,128]{1,0:T(8,128)(2,1)} %wk_in.1, ...), custom_call_target="tpu_custom_call" | custom-call | tf_op jit(solution)/shard_map/layer/pallas_call | solution.py:637
  131.5 2.0 %copy.12 = bf16[36,8192]{1,0:T(8,128)(2,1)} copy(bf16[36,8192]{1,0:T(8,128)(2,1)} %layer.1) | data formatting | bytes 1179648
